TPU v7x, 8 devices: a whole 2x2x1 slice. The times are simulated.
8 devices in a mesh: dp: 1 (over z), tp: 8 (over y, x, core).
Axes of the slice: x: 2, y: 2, z: 1, core: 2. Of those that a mesh axis runs over, the one named last changes fastest.
Arguments:
- x: bfloat16 [3072, 5120], P(('dp', 'tp'))
- dy: bfloat16 [3072, 5120], P(('dp', 'tp'))
- wg: bfloat16 [5120, 14336], P(None, 'tp')
- wu: bfloat16 [5120, 14336], P(None, 'tp')
- wd: bfloat16 [14336, 5120], P('tp')
- ug: bfloat16 [3072, 14336], P('dp', 'tp')
- uu: bfloat16 [3072, 14336], P('dp', 'tp')
Outputs:
- output 1: bfloat16 [3072, 5120], P(('dp', 'tp'))
- output 2: float32 [5120, 14336], P('dp', 'tp')
- output 3: float32 [5120, 14336], P('dp', 'tp')
- output 4: float32 [14336, 5120], P(('dp', 'tp'))
All inputs are finite; a program needn't handle non-finite values.
Results may differ from a plain program's by a relative error of at most 0.0116402.
Values are sent between devices in bfloat16 or wider.
A program may use at most 1 GiB of HBM per device.

v0:
```python
import jax
import jax.numpy as jnp
from jax import lax
from jax.sharding import PartitionSpec as P


def solution(mesh):
    tok = P(("dp", "tp"), None)
    col = P(None, "tp")
    row = P("tp", None)
    act = P("dp", "tp")

    def body(x, dy, wg, wu, wd, ug, uu):
        xg = lax.all_gather(x, "tp", axis=0, tiled=True)
        dyg = lax.all_gather(dy, "tp", axis=0, tiled=True)
        ug32 = ug.astype(jnp.float32)
        uu32 = uu.astype(jnp.float32)
        s = jax.nn.sigmoid(ug32)
        a = ug32 * s
        z = (a * uu32).astype(jnp.bfloat16)
        dwd = jnp.dot(z.T, dyg, preferred_element_type=jnp.float32)
        g = jnp.dot(dyg, wd.T, preferred_element_type=jnp.float32)
        duu = (g * a).astype(jnp.bfloat16)
        dug = (g * uu32 * s * (1.0 + ug32 * (1.0 - s))).astype(jnp.bfloat16)
        p = jnp.dot(dug, wg.T, preferred_element_type=jnp.float32) + jnp.dot(duu, wu.T, preferred_element_type=jnp.float32)
        dx = lax.psum_scatter(p.astype(jnp.bfloat16), "tp", scatter_dimension=0, tiled=True)
        dwg = jnp.dot(xg.T, dug, preferred_element_type=jnp.float32)
        dwu = jnp.dot(xg.T, duu, preferred_element_type=jnp.float32)
        return dx, dwg, dwu, dwd

    return jax.shard_map(body, mesh=mesh, in_specs=(tok, tok, col, col, row, act, act), out_specs=(tok, act, act, tok), check_vma=False)
```

profile of v0, /device:TPU:0, one launch (start us, length us, event | category | flops | bytes accessed | tf_op | source)
XLA Modules:
  0.0 693.4 jit_solution(551649283059547977)
XLA Ops:
  7.2 0.0 all-gather.3.cloned.1.call-start
  7.2 0.7 all-gather.3.cloned.1.call-update
  7.9 0.0 all-gather.5.cloned.1.call-start
  7.9 0.7 all-gather.5.cloned.1.call-update
  8.6 0.0 reduce-scatter.2.cloned.1.call-start
  8.7 150.2 %all-gather.3.cloned.1.call-done = bf16[3072,5120]{1,0:T(8,128)(2,1)} async-done(((bf16[384,5120]{1,0:T(8,128)(2,1)}), bf16[3072,5120]{1,0:T(8,128)(2,1)}) %all-gather.3.cloned.1.call-update) | async-done | bytes 31457296 | tf_op jit(solution)/shard_map/all_gather | solution.py:15
  158.9 80.5 %fusion.2 = (bf16[3072,1792]{1,0:T(8,128)(2,1)}, f32[3072,1792]{1,0:T(8,128)}) fusion(bf16[3072,1792]{1,0:T(8,128)(2,1)} %param.13, bf16[3072,1792]{1,0:T(8,128)(2,1)} %param.12, bf16[3072,5120]{1,0:T(8,128)(2,1)} %all-gather.3.cloned.1.call-done, bf16[1792,5120]{1,0:T(8,128)(2,1)} %param.11), kind=kOutput, calls=%fused_computation.8 | convolution fusion | flops 56437506048 | bytes 104857600 | tf_op jit(solution)/shard_map/dot_general | solution.py:22
  239.4 68.8 %fusion.11 = f32[3072,5120]{1,0:T(8,128)} fusion(bf16[3072,1792]{1,0:T(8,128)(2,1)} %get-tuple-element.8, bf16[5120,1792]{1,0:T(8,128)(2,1)} %param.9), kind=kOutput, calls=%fused_computation.19 | convolution fusion | flops 56371445760 | bytes 92274688 | tf_op jit(solution)/shard_map/dot_general | solution.py:25
  308.2 73.1 %add_convert_fusion = bf16[3072,5120]{1,0:T(8,128)(2,1)} fusion(f32[3072,5120]{1,0:T(8,128)} %fusion.11, bf16[5120,1792]{1,0:T(8,128)(2,1)} %param.10, f32[3072,1792]{1,0:T(8,128)} %get-tuple-element.9, bf16[3072,1792]{1,0:T(8,128)(2,1)} %param.12), kind=kOutput, calls=%fused_computation | convolution fusion | flops 56441438208 | bytes 145752064 | tf_op jit(solution)/shard_map/dot_general | solution.py:25
  381.4 0.0 reduce-scatter.2.cloned.1.call-update
  381.4 0.0 all-gather.5.cloned.1.call-done
  381.4 70.1 %convolution_bitcast_fusion.1 = f32[5120,1792]{0,1:T(8,128)} fusion(bf16[3072,1792]{1,0:T(8,128)(2,1)} %get-tuple-element.8, bf16[3072,5120]{1,0:T(8,128)(2,1)} %all-gather.5.cloned.1.call-done), kind=kOutput, calls=%fused_computation.16 | convolution fusion | flops 56371445760 | bytes 79167488 | tf_op jit(solution)/shard_map/dot_general | solution.py:27
  451.5 35.8 %copy.11 = f32[5120,1792]{1,0:T(8,128)} copy(f32[5120,1792]{0,1:T(8,128)} %convolution_bitcast_fusion.1) | data formatting | bytes 73400320
  487.3 77.4 %convolution_bitcast_fusion = f32[5120,1792]{0,1:T(8,128)} fusion(bf16[3072,5120]{1,0:T(8,128)(2,1)} %all-gather.5.cloned.1.call-done, f32[3072,1792]{1,0:T(8,128)} %get-tuple-element.9, bf16[3072,1792]{1,0:T(8,128)(2,1)} %param.12), kind=kOutput, calls=%fused_computation.15 | convolution fusion | flops 56409980928 | bytes 101187584 | tf_op jit(solution)/shard_map/dot_general | solution.py:28
  564.7 35.0 %copy.12 = f32[5120,1792]{1,0:T(8,128)} copy(f32[5120,1792]{0,1:T(8,128)} %convolution_bitcast_fusion) | data formatting | bytes 73400320
  599.6 87.1 %fusion.8 = f32[1792,5120]{1,0:T(8,128)} fusion(bf16[3072,5120]{1,0:T(8,128)(2,1)} %all-gather.3.cloned.1.call-done, bf16[3072,1792]{1,0:T(8,128)(2,1)} %param.13, bf16[3072,1792]{1,0:T(8,128)(2,1)} %param.12), kind=kOutput, calls=%fused_computation.17 | convolution fusion | flops 56415485952 | bytes 90177536 | tf_op jit(solution)/shard_map/dot_general | solution.py:21
  686.7 0.0 reduce-scatter.2.cloned.1.call-done
Async XLA Ops:
  7.2 151.7 %all-gather.3.cloned.1.call-start = ((), (), s32[]{:S(2)}) async-start(), calls=%async_computation.1 | async-start | bytes 35389440 | tf_op jit(solution)/shard_map/all_gather | solution.py:15
  7.9 373.5 %all-gather.5.cloned.1.call-start = ((), (), s32[]{:S(2)}) async-start(), calls=%async_computation.3 | async-start | bytes 35389440 | tf_op jit(solution)/shard_map/all_gather | solution.py:14
  8.6 678.1 %reduce-scatter.2.cloned.1.call-start = ((), (), s32[]{:S(2)}) async-start(), calls=%async_computation.2 | async-start | bytes 35389440 | tf_op jit(solution)/shard_map/reduce_scatter | solution.py:26
Sparse Core Ops, SparseCore 0:
  9.8 149.0 all-gather.2
  160.7 146.2 all-gather.4
  381.5 183.0 reduce-scatter.1
where the time goes:
time: 699 us; the launch traced here: 693 us
  matrix products  457 us (65%)
  waiting for transfers between devices  152 us (22%)
  local copies, waits for them, and re-layouts  70.8 us (10%)
  between operations  13.9 us (2%)
    all_gather x1, waiting for transfers between devices, body(): dyg = lax.all_gather(dy, 'tp', axis=0, tiled=True)  150 us
    dot_general x1, matrix products, body(): dwd = jnp.dot(z.T, dyg, preferred_element_type=jnp.float32)  87.1 us
    dot_general x1, matrix products, body(): g = jnp.dot(dyg, wd.T, preferred_element_type=jnp.float32)  80.5 us
    dot_general x1, matrix products, body(): dwu = jnp.dot(xg.T, duu, preferred_element_type=jnp.float32)  77.4 us
    dot_general x1, matrix products, body(): jnp.dot(duu, wu.T, preferred_element_type=jnp.float32)  73.1 us
    unnamed x2, local copies, waits for them, and re-layouts  70.8 us
    dot_general x1, matrix products, body(): dwg = jnp.dot(xg.T, dug, preferred_element_type=jnp.float32)  70.1 us
    dot_general x1, matrix products, body(): jnp.dot(dug, wg.T, preferred_element_type=jnp.float32)  68.8 us
  transfers between devices with their start and end apart: 3, of which 1 were waited for; matrix products, arithmetic and copies ran while one was open for 76% of the time, Pallas kernels for 0%

commit v1 on v0

v1 whole, which is shorter than its diff:
```python
import functools

import jax
import jax.numpy as jnp
from jax import lax
from jax.experimental import pallas as pl
from jax.experimental.pallas import tpu as pltpu
from jax.sharding import PartitionSpec as P


BF16 = jnp.bfloat16
F32 = jnp.float32
VMEM_LIMIT = 60 * 1024 * 1024
ANY = pl.BlockSpec(memory_space=pl.ANY)
NT = (((1,), (1,)), ((), ()))
TN = (((0,), (0,)), ((), ()))


def params():
    return pltpu.CompilerParams(vmem_limit_bytes=VMEM_LIMIT)


def cost(m, k, n, nbytes):
    return pl.CostEstimate(flops=2 * m * k * n, bytes_accessed=nbytes, transcendentals=0)


def gp_chunk(dys, wd, ug, uu, wg, wu, places):
    f, h = wd.shape
    total = sum(d.shape[0] for d in dys)
    shard = ug.shape[0] // 8
    half = total // 2
    bg, bp = 512, 512
    gsteps, psteps = f // bg, h // bp
    rest = f - gsteps * bg
    wide = (gsteps + 1) * bg
    nd, npc = len(dys), len(places)

    def kernel(*refs):
        dy_refs = refs[:nd]
        wd_ref, ug_ref, uu_ref, wg_ref, wu_ref = refs[nd : nd + 5]
        own_ref, oth_ref, dug_out, duu_out, zt_out = refs[nd + 5 : nd + 10]
        lhs, ugs, uus, dug, duu, zt, gs, lsem, usem, osem = refs[nd + 10 :]
        i = pl.program_id(0)
        me = lax.axis_index("tp")

        def lhs_copies():
            off, out = 0, []
            for j, d in enumerate(dy_refs):
                out.append(pltpu.make_async_copy(d, lhs.at[pl.ds(off, d.shape[0]), :], lsem.at[j]))
                off += d.shape[0]
            return out

        def u_copies():
            off, out = 0, []
            for j, (mask, first, rows) in enumerate(places):
                src = pl.ds(pl.multiple_of(jnp.bitwise_xor(me, mask) * shard + first, 64), rows)
                for k, (a, s) in enumerate(((ug_ref, ugs), (uu_ref, uus))):
                    dst = s.at[pl.ds(off, rows), pl.ds(0, f)]
                    out.append(pltpu.make_async_copy(a.at[src, :], dst, usem.at[k, j]))
                off += rows
            return out

        def out_copies():
            return [
                pltpu.make_async_copy(dug.at[:, pl.ds(0, f)], dug_out, osem.at[0]),
                pltpu.make_async_copy(duu.at[:, pl.ds(0, f)], duu_out, osem.at[1]),
                pltpu.make_async_copy(zt.at[pl.ds(0, f), :], zt_out, osem.at[2]),
            ]

        def epilogue(slot, col):
            cols = pl.ds(pl.multiple_of(col, bg), bg)
            for q in range(0, total, 128):
                r = pl.ds(q, 128)
                a32 = ugs[r, cols].astype(F32)
                u32 = uus[r, cols].astype(F32)
                s = 0.5 * jnp.tanh(0.5 * a32) + 0.5
                act = a32 * s
                g = gs[slot, r, :]
                duu[r, cols] = (g * act).astype(BF16)
                dug[r, cols] = (g * (u32 * s * (1.0 + a32 * (1.0 - s)))).astype(BF16)
                zt[cols, r] = (act * u32).astype(BF16).T

        @pl.when(i == 0)
        def _():
            for c in lhs_copies() + u_copies():
                c.start()
            for c in lhs_copies():
                c.wait()
            gs[0, :, pl.ds(0, rest)] = lax.dot_general(
                lhs[...], wd_ref[pl.ds(0, rest), :], NT, preferred_element_type=F32
            )
            for c in u_copies():
                c.wait()

        @pl.when((i > 0) & (i <= gsteps))
        def _():
            gs[lax.rem(i, 2)] = lax.dot_general(lhs[...], wd_ref[...], NT, preferred_element_type=F32)
            epilogue(lax.rem(i + 1, 2), jnp.where(i == 1, gsteps, i - 2) * bg)

        @pl.when(i == gsteps)
        def _():
            epilogue(gsteps % 2, (gsteps - 1) * bg)
            for c in out_copies():
                c.start()

        @pl.when(i > gsteps)
        def _():
            acc = lax.dot_general(dug[:, pl.ds(0, f)], wg_ref[...], NT, preferred_element_type=F32)
            acc += lax.dot_general(duu[:, pl.ds(0, f)], wu_ref[...], NT, preferred_element_type=F32)
            own_ref[...] = acc[:half].astype(BF16)
            oth_ref[...] = acc[half:].astype(BF16)

        @pl.when(i == gsteps + psteps)
        def _():
            for c in out_copies():
                c.wait()

    wd_block = lambda i: (jnp.where(i == 0, gsteps, jnp.minimum(i, gsteps) - 1), 0)
    p_block = lambda i: jnp.maximum(i - gsteps - 1, 0)
    return pl.pallas_call(
        kernel,
        grid=(gsteps + 1 + psteps,),
        in_specs=[ANY] * nd
        + [pl.BlockSpec((bg, h), wd_block), ANY, ANY]
        + [pl.BlockSpec((bp, f), lambda i: (p_block(i), 0))] * 2,
        out_specs=[pl.BlockSpec((half, bp), lambda i: (0, p_block(i)))] * 2 + [ANY] * 3,
        scratch_shapes=[
            pltpu.VMEM((total, h), BF16),
            pltpu.VMEM((total, wide), BF16),
            pltpu.VMEM((total, wide), BF16),
            pltpu.VMEM((total, wide), BF16),
            pltpu.VMEM((total, wide), BF16),
            pltpu.VMEM((wide, total), BF16),
            pltpu.VMEM((2, total, bg), F32),
            pltpu.SemaphoreType.DMA((nd,)),
            pltpu.SemaphoreType.DMA((2, npc)),
            pltpu.SemaphoreType.DMA((3,)),
        ],
        out_shape=[
            jax.ShapeDtypeStruct((half, h), BF16),
            jax.ShapeDtypeStruct((half, h), BF16),
            jax.ShapeDtypeStruct((total, f), BF16),
            jax.ShapeDtypeStruct((total, f), BF16),
            jax.ShapeDtypeStruct((f, total), BF16),
        ],
        compiler_params=params(),
        cost_estimate=cost(total, 3 * h, f, 2 * (3 * f * h + total * (2 * h + 5 * f))),
        name="gp_chunk",
    )(*dys, wd, ug, uu, wg, wu)


def dw(streamed, moves, resident, transposed):
    ns, nr = len(streamed), len(resident)
    nm = len(moves)
    h = streamed[0].shape[1]
    if transposed:
        tokens, f = sum(r.shape[0] for r in resident), resident[0].shape[1]
        res_shape = (tokens, f)
    else:
        tokens, f = sum(r.shape[1] for r in resident), resident[0].shape[0]
        res_shape = (f, tokens)
    bn = 512
    steps = h // bn

    def kernel(*refs):
        s_refs = refs[:ns]
        r_refs = refs[ns : ns + nr]
        out_ref, buf, res, sem, rsem = refs[ns + nr :]
        i = pl.program_id(0)
        slot = lax.rem(i, 2)

        def block(step, where):
            cols = pl.ds(pl.multiple_of(step * bn, bn), bn)
            return [
                pltpu.make_async_copy(
                    s_refs[a].at[pl.ds(src, n), cols], buf.at[where, pl.ds(dst, n), :], sem.at[where, m]
                )
                for m, (a, src, n, dst) in enumerate(moves)
            ]

        @pl.when(i == 0)
        def _():
            for c in block(0, 0):
                c.start()
            copies, off = [], 0
            for j, r in enumerate(r_refs):
                n = r.shape[0] if transposed else r.shape[1]
                dst = res.at[pl.ds(off, n), :] if transposed else res.at[:, pl.ds(off, n)]
                c = pltpu.make_async_copy(r, dst, rsem.at[j])
                c.start()
                copies.append(c)
                off += n
            for c in copies:
                c.wait()

        @pl.when(i + 1 < steps)
        def _():
            for c in block(i + 1, lax.rem(i + 1, 2)):
                c.start()

        for c in block(i, slot):
            c.wait()
        if transposed:
            out_ref[...] = lax.dot_general(buf[slot], res[...], TN, preferred_element_type=F32)
        else:
            out_ref[...] = jnp.dot(res[...], buf[slot], preferred_element_type=F32)

    if transposed:
        out_spec, out_shape = pl.BlockSpec((bn, f), lambda i: (i, 0)), (h, f)
    else:
        out_spec, out_shape = pl.BlockSpec((f, bn), lambda i: (0, i)), (f, h)
    return pl.pallas_call(
        kernel,
        grid=(steps,),
        in_specs=[ANY] * (ns + nr),
        out_specs=out_spec,
        out_shape=jax.ShapeDtypeStruct(out_shape, F32),
        scratch_shapes=[
            pltpu.VMEM((2, tokens, bn), BF16),
            pltpu.VMEM(res_shape, BF16),
            pltpu.SemaphoreType.DMA((2, nm)),
            pltpu.SemaphoreType.DMA((nr,)),
        ],
        compiler_params=params(),
        cost_estimate=cost(tokens, h, f, 2 * tokens * (h + f) + 4 * h * f),
        name="dw",
    )(*streamed, *resident)


def solution(mesh):
    tok = P(("dp", "tp"), None)
    col = P(None, "tp")
    row = P("tp", None)
    act = P("dp", "tp")
    n = mesh.shape["tp"]
    pairs = {m: [(i, i ^ m) for i in range(n)] for m in (1, 2, 4)}
    core, xn, yn = pairs[1], pairs[2], pairs[4]

    def send(a, to):
        return lax.ppermute(a, "tp", to)

    def add(*terms):
        return functools.reduce(lambda a, b: a + b, [t.astype(F32) for t in terms]).astype(BF16)

    def inner(x, dy, wg, wu, wd, ug, uu):
        t = x.shape[0]
        u = t // 2
        dyp = [dy[:u], dy[u:]]
        dyc = send(dy, core)
        dyx0 = send(dyp[0], xn)
        dyy1 = send(dyp[1], yn)
        dyx1 = send(dyp[1], xn)
        dyy0 = send(dyp[0], yn)
        dyxc0, dyyc1 = send(dyx0, core), send(dyy1, core)
        dyd0, dyd1 = send(dyx0, yn), send(dyy1, xn)
        dyxc1, dyyc0 = send(dyx1, core), send(dyy0, core)
        dydc0, dydc1 = send(dyd0, core), send(dyd1, core)
        xx, xy, xc = send(x, xn), send(x, yn), send(x, core)
        xd0, xd1 = send(xx[:u], yn), send(xy[u:], xn)
        xxc, xyc = send(xx, core), send(xy, core)
        xdc0, xdc1 = send(xd0, core), send(xd1, core)

        chunks = (
            ([dy, dyc], [(0, 0, t), (1, 0, t)]),
            ([dyx0, dyy1, dyxc0, dyyc1], [(2, 0, u), (4, u, u), (3, 0, u), (5, u, u)]),
            ([dyx1, dyy0, dyxc1, dyyc0], [(2, u, u), (4, 0, u), (3, u, u), (5, 0, u)]),
            ([dyd0, dyd1, dydc0, dydc1], [(6, 0, t), (7, 0, t)]),
        )
        own, oth, dug, duu, zt = [], [], [], [], []
        for rows, places in chunks:
            res = gp_chunk(rows, wd, ug, uu, wg, wu, places)
            for dst, r in zip((own, oth, dug, duu, zt), res):
                dst.append(r)
        got = [send(oth[c], core) for c in range(4)]
        mine = lambda c, j: (own[c][j * u : (j + 1) * u], got[c][j * u : (j + 1) * u])
        rdx = send(add(*mine(3, 0)), xn)
        rdy = send(add(*mine(3, 1)), yn)
        rx0 = send(add(*mine(1, 0)), xn)
        ry1 = send(add(*mine(1, 1)), yn)
        rx1 = send(add(*mine(2, 0), rdy), xn)
        ry0 = send(add(*mine(2, 1), rdx), yn)
        dx = jnp.concatenate([add(*mine(0, 0), rx0, ry0), add(*mine(0, 1), rx1, ry1)])

        def moves(parts):
            out, dst = [], 0
            for a, src, rows in parts:
                out.append((a, src, rows, dst))
                dst += rows
            return out

        dy_arrays = [a for rows, _ in chunks for a in rows]
        dy_moves = moves([(k, 0, a.shape[0]) for k, a in enumerate(dy_arrays)])
        dwd = dw(dy_arrays, dy_moves, zt, False)
        x_arrays = [x, xc, xx, xy, xxc, xyc, xd0, xd1, xdc0, xdc1]
        x_moves = moves(
            [(0, 0, t), (1, 0, t), (2, 0, u), (3, u, u), (4, 0, u), (5, u, u), (2, u, u), (3, 0, u), (4, u, u), (5, 0, u)]
            + [(k, 0, u) for k in (6, 7, 8, 9)]
        )
        dwg = dw(x_arrays, x_moves, dug, True)
        dwu = dw(x_arrays, x_moves, duu, True)
        return dx, dwg, dwu, dwd

    return jax.shard_map(
        inner, mesh=mesh, in_specs=(tok, tok, col, col, row, act, act), out_specs=(tok, act, act, tok), check_vma=False
    )
```

time: 699 us -> 621 us (0.89)
  matrix products: 457 us -> 0 us
  Pallas kernels: 0 us -> 441 us
  local copies, waits for them, and re-layouts: 70.8 us -> 5.76 us
  waiting for transfers between devices: 152 us -> 120 us
  other arithmetic: 0 us -> 24.9 us
  starting transfers between devices: 0.11 us -> 21.6 us
  between operations: 13.9 us -> 1.35 us
    dot_general x6 -> x0, matrix products: 457 us -> none  [the longest x1 87.1 us: body(): dwd = jnp.dot(z.T, dyg, preferred_element_type=jnp.float32)]
    pallas_call x0 -> x7, Pallas kernels: none -> 441 us  [the longest x4 240 us: gp_chunk(): pl.pallas_call(kernel, grid=(gsteps + 1 + psteps,), in_specs=[ANY] * nd +...]
    all_gather x2 -> x0, waiting for transfers between devices: 150 us -> none  [the longest x1 150 us: body(): dyg = lax.all_gather(dy, 'tp', axis=0, tiled=True)]
    ppermute x0 -> x32, waiting for transfers between devices: none -> 120 us  [send(): return lax.ppermute(a, 'tp', to)]
    unnamed x2 -> x12, local copies, waits for them, and re-layouts: 70.8 us -> 0.02 us
    convert_element_type x0 -> x4, other arithmetic: none -> 22.7 us  [add(): functools.reduce(lambda a, b: a + b, [t.astype(F32) for t in terms])]
    ppermute x0 -> x32, starting transfers between devices: none -> 21.6 us  [send(): return lax.ppermute(a, 'tp', to)]
  transfers between devices with their start and end apart: 3 -> 32, of which waited for: 1 -> 3; matrix products, arithmetic and copies ran while one was open for 76% -> 4% of each run, Pallas kernels for 0% -> 72%
where the time goes in v1:
time: 621 us; the launch traced here: 615 us
  Pallas kernels  441 us (71%)
  waiting for transfers between devices  120 us (19%)
  other arithmetic  24.9 us (4%)
  starting transfers between devices  21.6 us (3%)
    pallas_call x4, Pallas kernels, gp_chunk(): pl.pallas_call(kernel, grid=(gsteps + 1 + psteps,), in_specs=[ANY] * nd +...  240 us
    pallas_call x3, Pallas kernels, dw(): pl.pallas_call(kernel, grid=(steps,), in_specs=[ANY] * (ns + nr), out_spe...  202 us
    ppermute x32, waiting for transfers between devices, send(): return lax.ppermute(a, 'tp', to)  120 us
    convert_element_type x4, other arithmetic, add(): functools.reduce(lambda a, b: a + b, [t.astype(F32) for t in terms])  22.7 us
    ppermute x32, starting transfers between devices, send(): return lax.ppermute(a, 'tp', to)  21.6 us
  transfers between devices with their start and end apart: 32, of which 3 were waited for; matrix products, arithmetic and copies ran while one was open for 4% of the time, Pallas kernels for 72%

profile of v1, /device:TPU:0, one launch (start us, length us, event | category | flops | bytes accessed | tf_op | source)
XLA Modules:
  0.0 615.0 jit_solution(3220512803362399411)
XLA Ops:
  0.6 0.9 collective-permute-start
  1.5 2.4 fusion
  3.9 2.5 collective-permute-start.3
  6.4 1.5 collective-permute-start.2
  7.9 0.5 collective-permute-start.8
  8.5 41.7 %collective-permute-done.3.refs_1_.refs_3_ = bf16[192,5120]{1,0:T(8,128)(2,1)} collective-permute-done((bf16[192,5120]{1,0:T(8,128)(2,1)S(1)}, bf16[192,5120]{1,0:T(8,128)(2,1)}, u32[]{:S(2)}, u32[]{:S(2)}) %collective-permute-start.3) | collective-permute-done | bytes 1966112 | tf_op jit(solution)/shard_map/ppermute | solution.py:240
  50.2 2.0 collective-permute-start.25
  52.2 0.5 collective-permute-start.4
  52.7 59.3 %gp_chunk.4 = (bf16[384,5120]{1,0:T(8,128)(2,1)}, bf16[384,5120]{1,0:T(8,128)(2,1)}, bf16[768,1792]{1,0:T(8,128)(2,1)}, bf16[768,1792]{1,0:T(8,128)(2,1)}, bf16[1792,768]{1,0:T(8,128)(2,1)}) custom-call(bf16[384,5120]{1,0:T(8,128)(2,1)} %refs_0_.7, bf16[384,5120]{1,0:T(8,128)(2,1)} %collective-permute-done.refs_1_, bf16[1792,5120]{1,0:T(8,128)(2,1)} %refs_4_.7, ...), custom_call_target="tpu_custom_call" | custom-call | flops 42278584320 | bytes 84541440 | tf_op jit(solution)/shard_map/gp_chunk/pallas_call | solution.py:120
  112.1 1.5 collective-permute-start.24
  113.6 0.5 collective-permute-start.14
  114.2 62.4 %collective-permute-done.25.refs_3_ = bf16[384,5120]{1,0:T(8,128)(2,1)} collective-permute-done((bf16[384,5120]{1,0:T(8,128)(2,1)}, bf16[384,5120]{1,0:T(8,128)(2,1)}, u32[]{:S(2)}, u32[]{:S(2)}) %collective-permute-start.25) | collective-permute-done | bytes 3932192 | tf_op jit(solution)/shard_map/ppermute | solution.py:240
  176.6 60.4 %gp_chunk.5 = (bf16[384,5120]{1,0:T(8,128)(2,1)}, bf16[384,5120]{1,0:T(8,128)(2,1)}, bf16[768,1792]{1,0:T(8,128)(2,1)}, bf16[768,1792]{1,0:T(8,128)(2,1)}, bf16[1792,768]{1,0:T(8,128)(2,1)}) custom-call(bf16[192,5120]{1,0:T(8,128)(2,1)} %collective-permute-done.2.refs_0_.refs_2_, bf16[192,5120]{1,0:T(8,128)(2,1)} %collective-permute-done.3.refs_1_.refs_3_, ...), custom_call_target="tpu_custom_call" | custom-call | flops 42278584320 | bytes 84541440 | tf_op jit(solution)/shard_map/gp_chunk/pallas_call | solution.py:120
  237.1 1.7 slice.89
  238.7 0.5 collective-permute-start.23
  239.3 1.7 slice.88
  240.9 2.0 collective-permute-start.29
  243.0 1.5 collective-permute-start.28
  245.0 60.1 %gp_chunk.6 = (bf16[384,5120]{1,0:T(8,128)(2,1)}, bf16[384,5120]{1,0:T(8,128)(2,1)}, bf16[768,1792]{1,0:T(8,128)(2,1)}, bf16[768,1792]{1,0:T(8,128)(2,1)}, bf16[1792,768]{1,0:T(8,128)(2,1)}) custom-call(bf16[192,5120]{1,0:T(8,128)(2,1)} %collective-permute-done.8.refs_0_.refs_6_, bf16[192,5120]{1,0:T(8,128)(2,1)} %collective-permute-done.9.refs_1_.refs_7_, ...), custom_call_target="tpu_custom_call" | custom-call | flops 42278584320 | bytes 84541440 | tf_op jit(solution)/shard_map/gp_chunk/pallas_call | solution.py:120
  305.6 59.9 %gp_chunk.7 = (bf16[384,5120]{1,0:T(8,128)(2,1)}, bf16[384,5120]{1,0:T(8,128)(2,1)}, bf16[768,1792]{1,0:T(8,128)(2,1)}, bf16[768,1792]{1,0:T(8,128)(2,1)}, bf16[1792,768]{1,0:T(8,128)(2,1)}) custom-call(bf16[192,5120]{1,0:T(8,128)(2,1)} %collective-permute-done.13.refs_0_.refs_10_, bf16[192,5120]{1,0:T(8,128)(2,1)} %collective-permute-done.14.refs_1_.refs_11_, ...), custom_call_target="tpu_custom_call" | custom-call | flops 42278584320 | bytes 84541440 | tf_op jit(solution)/shard_map/gp_chunk/pallas_call | solution.py:120
  366.1 67.3 %dw.5 = f32[1792,5120]{1,0:T(8,128)} custom-call(bf16[384,5120]{1,0:T(8,128)(2,1)} %refs_0_.7, bf16[384,5120]{1,0:T(8,128)(2,1)} %collective-permute-done.refs_1_, bf16[192,5120]{1,0:T(8,128)(2,1)} %collective-permute-done.2.refs_0_.refs_2_, bf16[192,5120]{1,0:T(8,128)(2,1)} %collective-permute-done.3.refs_1_.refs_3_, ...), custom_call_target="tpu_custom_call" | custom-call | flops 56371445760 | bytes 79167488 | tf_op jit(solution)/shard_map/dw/pallas_call | solution.py:212
  433.9 5.7 add_convert_fusion.7
  439.6 5.5 add_convert_fusion.6
  445.6 0.6 collective-permute-start.7
  446.2 1.4 collective-permute-start.18
  448.1 67.1 %dw.3 = f32[5120,1792]{1,0:T(8,128)} custom-call(bf16[384,5120]{1,0:T(8,128)(2,1)} %refs_0_.6, bf16[384,5120]{1,0:T(8,128)(2,1)} %collective-permute-done.23.refs_1_, bf16[384,5120]{1,0:T(8,128)(2,1)} %collective-permute-done.24.refs_2_, bf16[384,5120]{1,0:T(8,128)(2,1)} %collective-permute-done.25.refs_3_, ...), custom_call_target="tpu_custom_call" | custom-call | flops 56371445760 | bytes 79167488 | tf_op jit(solution)/shard_map/dw/pallas_call | solution.py:212
  515.3 1.6 collective-permute-start.22
  516.9 16.0 %collective-permute-done.18 = bf16[192,5120]{1,0:T(8,128)(2,1)} collective-permute-done((bf16[192,5120]{1,0:T(8,128)(2,1)}, bf16[192,5120]{1,0:T(8,128)(2,1)}, u32[]{:S(2)}, u32[]{:S(2)}) %collective-permute-start.18) | collective-permute-done | bytes 1966112 | tf_op jit(solution)/shard_map/ppermute | solution.py:240
  532.9 5.8 add_convert_fusion.5
  539.5 67.1 %dw.4 = f32[5120,1792]{1,0:T(8,128)} custom-call(bf16[384,5120]{1,0:T(8,128)(2,1)} %refs_0_.6, bf16[384,5120]{1,0:T(8,128)(2,1)} %collective-permute-done.23.refs_1_, bf16[384,5120]{1,0:T(8,128)(2,1)} %collective-permute-done.24.refs_2_, bf16[384,5120]{1,0:T(8,128)(2,1)} %collective-permute-done.25.refs_3_, ...), custom_call_target="tpu_custom_call" | custom-call | flops 56371445760 | bytes 79167488 | tf_op jit(solution)/shard_map/dw/pallas_call | solution.py:212
  606.6 5.7 add_convert_fusion.4
  612.3 2.2 pad_maximum_fusion
  (59 shorter events, 4.0 us)
Async XLA Ops:
  0.6 51.6 %collective-permute-start = (bf16[384,5120]{1,0:T(8,128)(2,1)}, bf16[384,5120]{1,0:T(8,128)(2,1)}, u32[]{:S(2)}, u32[]{:S(2)}) collective-permute-start(bf16[384,5120]{1,0:T(8,128)(2,1)} %refs_0_.7), channel_id=1, source_target_pairs={{0,1},{1,0},{2,3},{3,2},{4,5},{5,4},{6,7},{7,6}} | collective-permute-start | bytes 11796488 | tf_op jit(solution)/shard_map/ppermute | solution.py:240
  3.9 46.3 %collective-permute-start.3 = (bf16[192,5120]{1,0:T(8,128)(2,1)S(1)}, bf16[192,5120]{1,0:T(8,128)(2,1)}, u32[]{:S(2)}, u32[]{:S(2)}) collective-permute-start(bf16[192,5120]{1,0:T(8,128)(2,1)S(1)} %get-tuple-element.52), channel_id=1, source_target_pairs={{0,4},{1,5},{2,6},{3,7},{4,0},{5,1},{6,2},{7,3}} | collective-permute-start | bytes 5898248 | tf_op jit(solution)/shard_map/ppermute | solution.py:240
  6.4 45.8 %collective-permute-start.2 = (bf16[192,5120]{1,0:T(8,128)(2,1)S(1)}, bf16[192,5120]{1,0:T(8,128)(2,1)}, u32[]{:S(2)}, u32[]{:S(2)}) collective-permute-start(bf16[192,5120]{1,0:T(8,128)(2,1)S(1)} %get-tuple-element.53), channel_id=1, source_target_pairs={{0,2},{1,3},{2,0},{3,1},{4,6},{5,7},{6,4},{7,5}} | collective-permute-start | bytes 5898248 | tf_op jit(solution)/shard_map/ppermute | solution.py:240
  7.9 104.1 %collective-permute-start.8 = (bf16[192,5120]{1,0:T(8,128)(2,1)S(1)}, bf16[192,5120]{1,0:T(8,128)(2,1)}, u32[]{:S(2)}, u32[]{:S(2)}) collective-permute-start(bf16[192,5120]{1,0:T(8,128)(2,1)S(1)} %get-tuple-element.52), channel_id=1, source_target_pairs={{0,2},{1,3},{2,0},{3,1},{4,6},{5,7},{6,4},{7,5}} | collective-permute-start | bytes 5898248 | tf_op jit(solution)/shard_map/ppermute | solution.py:240
  8.4 105.1 %collective-permute-start.9 = (bf16[192,5120]{1,0:T(8,128)(2,1)S(1)}, bf16[192,5120]{1,0:T(8,128)(2,1)}, u32[]{:S(2)}, u32[]{:S(2)}) collective-permute-start(bf16[192,5120]{1,0:T(8,128)(2,1)S(1)} %get-tuple-element.53), channel_id=1, source_target_pairs={{0,4},{1,5},{2,6},{3,7},{4,0},{5,1},{6,2},{7,3}} | collective-permute-start | bytes 5898248 | tf_op jit(solution)/shard_map/ppermute | solution.py:240
  50.2 126.4 %collective-permute-start.25 = (bf16[384,5120]{1,0:T(8,128)(2,1)}, bf16[384,5120]{1,0:T(8,128)(2,1)}, u32[]{:S(2)}, u32[]{:S(2)}) collective-permute-start(bf16[384,5120]{1,0:T(8,128)(2,1)} %refs_0_.6), channel_id=1, source_target_pairs={{0,4},{1,5},{2,6},{3,7},{4,0},{5,1},{6,2},{7,3}} | collective-permute-start | bytes 11796488 | tf_op jit(solution)/shard_map/ppermute | solution.py:240
  52.2 61.9 %collective-permute-start.5 = (bf16[192,5120]{1,0:T(8,128)(2,1)}, bf16[192,5120]{1,0:T(8,128)(2,1)}, u32[]{:S(2)}, u32[]{:S(2)}) collective-permute-start(bf16[192,5120]{1,0:T(8,128)(2,1)} %collective-permute-done.3.refs_1_.refs_3_), channel_id=1, source_target_pairs={{0,1},{1,0},{2,3},{3,2},{4,5},{5,4},{6,7},{7,6}} | collective-permute-start | bytes 5898248 | tf_op jit(solution)/shard_map/ppermute | solution.py:240
  52.2 61.9 %collective-permute-start.4 = (bf16[192,5120]{1,0:T(8,128)(2,1)}, bf16[192,5120]{1,0:T(8,128)(2,1)}, u32[]{:S(2)}, u32[]{:S(2)}) collective-permute-start(bf16[192,5120]{1,0:T(8,128)(2,1)} %collective-permute-done.2.refs_0_.refs_2_), channel_id=1, source_target_pairs={{0,1},{1,0},{2,3},{3,2},{4,5},{5,4},{6,7},{7,6}} | collective-permute-start | bytes 5898248 | tf_op jit(solution)/shard_map/ppermute | solution.py:240
  112.1 126.7 %collective-permute-start.24 = (bf16[384,5120]{1,0:T(8,128)(2,1)}, bf16[384,5120]{1,0:T(8,128)(2,1)}, u32[]{:S(2)}, u32[]{:S(2)}) collective-permute-start(bf16[384,5120]{1,0:T(8,128)(2,1)} %refs_0_.6), channel_id=1, source_target_pairs={{0,2},{1,3},{2,0},{3,1},{4,6},{5,7},{6,4},{7,5}} | collective-permute-start | bytes 11796488 | tf_op jit(solution)/shard_map/ppermute | solution.py:240
  113.6 129.4 %collective-permute-start.14 = (bf16[192,5120]{1,0:T(8,128)(2,1)}, bf16[192,5120]{1,0:T(8,128)(2,1)}, u32[]{:S(2)}, u32[]{:S(2)}) collective-permute-start(bf16[192,5120]{1,0:T(8,128)(2,1)} %collective-permute-done.3.refs_1_.refs_3_), channel_id=1, source_target_pairs={{0,2},{1,3},{2,0},{3,1},{4,6},{5,7},{6,4},{7,5}} | collective-permute-start | bytes 5898248 | tf_op jit(solution)/shard_map/ppermute | solution.py:240
  114.1 130.4 %collective-permute-start.13 = (bf16[192,5120]{1,0:T(8,128)(2,1)}, bf16[192,5120]{1,0:T(8,128)(2,1)}, u32[]{:S(2)}, u32[]{:S(2)}) collective-permute-start(bf16[192,5120]{1,0:T(8,128)(2,1)} %collective-permute-done.2.refs_0_.refs_2_), channel_id=1, source_target_pairs={{0,4},{1,5},{2,6},{3,7},{4,0},{5,1},{6,2},{7,3}} | collective-permute-start | bytes 5898248 | tf_op jit(solution)/shard_map/ppermute | solution.py:240
  114.2 126.8 %collective-permute-start.10 = (bf16[192,5120]{1,0:T(8,128)(2,1)}, bf16[192,5120]{1,0:T(8,128)(2,1)}, u32[]{:S(2)}, u32[]{:S(2)}) collective-permute-start(bf16[192,5120]{1,0:T(8,128)(2,1)} %collective-permute-done.8.refs_0_.refs_6_), channel_id=1, source_target_pairs={{0,1},{1,0},{2,3},{3,2},{4,5},{5,4},{6,7},{7,6}} | collective-permute-start | bytes 5898248 | tf_op jit(solution)/shard_map/ppermute | solution.py:240
  176.6 67.9 %collective-permute-start.11 = (bf16[192,5120]{1,0:T(8,128)(2,1)}, bf16[192,5120]{1,0:T(8,128)(2,1)}, u32[]{:S(2)}, u32[]{:S(2)}) collective-permute-start(bf16[192,5120]{1,0:T(8,128)(2,1)} %collective-permute-done.9.refs_1_.refs_7_), channel_id=1, source_target_pairs={{0,1},{1,0},{2,3},{3,2},{4,5},{5,4},{6,7},{7,6}} | collective-permute-start | bytes 5898248 | tf_op jit(solution)/shard_map/ppermute | solution.py:240
  238.7 206.4 %collective-permute-start.23 = (bf16[384,5120]{1,0:T(8,128)(2,1)}, bf16[384,5120]{1,0:T(8,128)(2,1)}, u32[]{:S(2)}, u32[]{:S(2)}) collective-permute-start(bf16[384,5120]{1,0:T(8,128)(2,1)} %refs_0_.6), channel_id=1, source_target_pairs={{0,1},{1,0},{2,3},{3,2},{4,5},{5,4},{6,7},{7,6}} | collective-permute-start | bytes 11796488 | tf_op jit(solution)/shard_map/ppermute | solution.py:240
  240.9 124.6 %collective-permute-start.29 = (bf16[192,5120]{1,0:T(8,128)(2,1)S(1)}, bf16[192,5120]{1,0:T(8,128)(2,1)}, u32[]{:S(2)}, u32[]{:S(2)}) collective-permute-start(bf16[192,5120]{1,0:T(8,128)(2,1)S(1)} %slice.89), channel_id=1, source_target_pairs={{0,2},{1,3},{2,0},{3,1},{4,6},{5,7},{6,4},{7,5}} | collective-permute-start | bytes 5898248 | tf_op jit(solution)/shard_map/ppermute | solution.py:240
  243.0 122.6 %collective-permute-start.28 = (bf16[192,5120]{1,0:T(8,128)(2,1)S(1)}, bf16[192,5120]{1,0:T(8,128)(2,1)}, u32[]{:S(2)}, u32[]{:S(2)}) collective-permute-start(bf16[192,5120]{1,0:T(8,128)(2,1)S(1)} %slice.88), channel_id=1, source_target_pairs={{0,4},{1,5},{2,6},{3,7},{4,0},{5,1},{6,2},{7,3}} | collective-permute-start | bytes 5898248 | tf_op jit(solution)/shard_map/ppermute | solution.py:240
  244.5 60.6 %collective-permute-start.16 = (bf16[192,5120]{1,0:T(8,128)(2,1)}, bf16[192,5120]{1,0:T(8,128)(2,1)}, u32[]{:S(2)}, u32[]{:S(2)}) collective-permute-start(bf16[192,5120]{1,0:T(8,128)(2,1)} %collective-permute-done.14.refs_1_.refs_11_), channel_id=1, source_target_pairs={{0,1},{1,0},{2,3},{3,2},{4,5},{5,4},{6,7},{7,6}} | collective-permute-start | bytes 5898248 | tf_op jit(solution)/shard_map/ppermute | solution.py:240
  244.5 60.7 %collective-permute-start.15 = (bf16[192,5120]{1,0:T(8,128)(2,1)}, bf16[192,5120]{1,0:T(8,128)(2,1)}, u32[]{:S(2)}, u32[]{:S(2)}) collective-permute-start(bf16[192,5120]{1,0:T(8,128)(2,1)} %collective-permute-done.13.refs_0_.refs_10_), channel_id=1, source_target_pairs={{0,1},{1,0},{2,3},{3,2},{4,5},{5,4},{6,7},{7,6}} | collective-permute-start | bytes 5898248 | tf_op jit(solution)/shard_map/ppermute | solution.py:240
  305.1 128.2 %collective-permute-start.6 = (bf16[384,5120]{1,0:T(8,128)(2,1)}, bf16[384,5120]{1,0:T(8,128)(2,1)}, u32[]{:S(2)}, u32[]{:S(2)}) collective-permute-start(bf16[384,5120]{1,0:T(8,128)(2,1)} %get-tuple-element.27), channel_id=1, source_target_pairs={{0,1},{1,0},{2,3},{3,2},{4,5},{5,4},{6,7},{7,6}} | collective-permute-start | bytes 11796488 | tf_op jit(solution)/shard_map/ppermute | solution.py:240
  305.2 140.5 %collective-permute-start.27 = (bf16[384,5120]{1,0:T(8,128)(2,1)}, bf16[384,5120]{1,0:T(8,128)(2,1)}, u32[]{:S(2)}, u32[]{:S(2)}) collective-permute-start(bf16[384,5120]{1,0:T(8,128)(2,1)} %collective-permute-done.25.refs_3_), channel_id=1, source_target_pairs={{0,1},{1,0},{2,3},{3,2},{4,5},{5,4},{6,7},{7,6}} | collective-permute-start | bytes 11796488 | tf_op jit(solution)/shard_map/ppermute | solution.py:240
  365.5 82.2 %collective-permute-start.26 = (bf16[384,5120]{1,0:T(8,128)(2,1)}, bf16[384,5120]{1,0:T(8,128)(2,1)}, u32[]{:S(2)}, u32[]{:S(2)}) collective-permute-start(bf16[384,5120]{1,0:T(8,128)(2,1)} %collective-permute-done.24.refs_2_), channel_id=1, source_target_pairs={{0,1},{1,0},{2,3},{3,2},{4,5},{5,4},{6,7},{7,6}} | collective-permute-start | bytes 11796488 | tf_op jit(solution)/shard_map/ppermute | solution.py:240
  365.6 67.8 %collective-permute-start.17 = (bf16[384,5120]{1,0:T(8,128)(2,1)}, bf16[384,5120]{1,0:T(8,128)(2,1)}, u32[]{:S(2)}, u32[]{:S(2)}) collective-permute-start(bf16[384,5120]{1,0:T(8,128)(2,1)} %get-tuple-element.31), channel_id=1, source_target_pairs={{0,1},{1,0},{2,3},{3,2},{4,5},{5,4},{6,7},{7,6}} | collective-permute-start | bytes 11796488 | tf_op jit(solution)/shard_map/ppermute | solution.py:240
  433.3 11.8 %collective-permute-start.31 = (bf16[192,5120]{1,0:T(8,128)(2,1)}, bf16[192,5120]{1,0:T(8,128)(2,1)S(1)}, u32[]{:S(2)}, u32[]{:S(2)}) collective-permute-start(bf16[192,5120]{1,0:T(8,128)(2,1)} %collective-permute-done.29.refs_7_), channel_id=1, source_target_pairs={{0,1},{1,0},{2,3},{3,2},{4,5},{5,4},{6,7},{7,6}} | collective-permute-start | bytes 5898248 | tf_op jit(solution)/shard_map/ppermute | solution.py:240
  433.4 12.8 %collective-permute-start.30 = (bf16[192,5120]{1,0:T(8,128)(2,1)}, bf16[192,5120]{1,0:T(8,128)(2,1)S(1)}, u32[]{:S(2)}, u32[]{:S(2)}) collective-permute-start(bf16[192,5120]{1,0:T(8,128)(2,1)} %collective-permute-done.28.refs_6_), channel_id=1, source_target_pairs={{0,1},{1,0},{2,3},{3,2},{4,5},{5,4},{6,7},{7,6}} | collective-permute-start | bytes 5898248 | tf_op jit(solution)/shard_map/ppermute | solution.py:240
  445.1 161.5 %collective-permute-start.1 = (bf16[384,5120]{1,0:T(8,128)(2,1)}, bf16[384,5120]{1,0:T(8,128)(2,1)}, u32[]{:S(2)}, u32[]{:S(2)}) collective-permute-start(bf16[384,5120]{1,0:T(8,128)(2,1)} %get-tuple-element.25), channel_id=1, source_target_pairs={{0,1},{1,0},{2,3},{3,2},{4,5},{5,4},{6,7},{7,6}} | collective-permute-start | bytes 11796488 | tf_op jit(solution)/shard_map/ppermute | solution.py:240
  445.2 70.1 %collective-permute-start.12 = (bf16[384,5120]{1,0:T(8,128)(2,1)}, bf16[384,5120]{1,0:T(8,128)(2,1)}, u32[]{:S(2)}, u32[]{:S(2)}) collective-permute-start(bf16[384,5120]{1,0:T(8,128)(2,1)} %get-tuple-element.29), channel_id=1, source_target_pairs={{0,1},{1,0},{2,3},{3,2},{4,5},{5,4},{6,7},{7,6}} | collective-permute-start | bytes 11796488 | tf_op jit(solution)/shard_map/ppermute | solution.py:240
  445.6 161.0 %collective-permute-start.7 = (bf16[192,5120]{1,0:T(8,128)(2,1)}, bf16[192,5120]{1,0:T(8,128)(2,1)}, u32[]{:S(2)}, u32[]{:S(2)}) collective-permute-start(bf16[192,5120]{1,0:T(8,128)(2,1)} %get-tuple-element.46), channel_id=1, source_target_pairs={{0,2},{1,3},{2,0},{3,1},{4,6},{5,7},{6,4},{7,5}} | collective-permute-start | bytes 5898248 | tf_op jit(solution)/shard_map/ppermute | solution.py:240
  446.2 86.6 %collective-permute-start.18 = (bf16[192,5120]{1,0:T(8,128)(2,1)}, bf16[192,5120]{1,0:T(8,128)(2,1)}, u32[]{:S(2)}, u32[]{:S(2)}) collective-permute-start(bf16[192,5120]{1,0:T(8,128)(2,1)} %get-tuple-element.50), channel_id=1, source_target_pairs={{0,2},{1,3},{2,0},{3,1},{4,6},{5,7},{6,4},{7,5}} | collective-permute-start | bytes 5898248 | tf_op jit(solution)/shard_map/ppermute | solution.py:240
  447.7 85.2 %collective-permute-start.20 = (bf16[192,5120]{1,0:T(8,128)(2,1)}, bf16[192,5120]{1,0:T(8,128)(2,1)}, u32[]{:S(2)}, u32[]{:S(2)}) collective-permute-start(bf16[192,5120]{1,0:T(8,128)(2,1)} %get-tuple-element.51), channel_id=1, source_target_pairs={{0,4},{1,5},{2,6},{3,7},{4,0},{5,1},{6,2},{7,3}} | collective-permute-start | bytes 5898248 | tf_op jit(solution)/shard_map/ppermute | solution.py:240
  515.3 91.3 %collective-permute-start.22 = (bf16[192,5120]{1,0:T(8,128)(2,1)}, bf16[192,5120]{1,0:T(8,128)(2,1)}, u32[]{:S(2)}, u32[]{:S(2)}) collective-permute-start(bf16[192,5120]{1,0:T(8,128)(2,1)} %get-tuple-element.47), channel_id=1, source_target_pairs={{0,4},{1,5},{2,6},{3,7},{4,0},{5,1},{6,2},{7,3}} | collective-permute-start | bytes 5898248 | tf_op jit(solution)/shard_map/ppermute | solution.py:240
  538.7 67.9 %collective-permute-start.19 = (bf16[192,5120]{1,0:T(8,128)(2,1)}, bf16[192,5120]{1,0:T(8,128)(2,1)}, u32[]{:S(2)}, u32[]{:S(2)}) collective-permute-start(bf16[192,5120]{1,0:T(8,128)(2,1)} %get-tuple-element.48), channel_id=1, source_target_pairs={{0,4},{1,5},{2,6},{3,7},{4,0},{5,1},{6,2},{7,3}} | collective-permute-start | bytes 5898248 | tf_op jit(solution)/shard_map/ppermute | solution.py:240
  539.2 67.5 %collective-permute-start.21 = (bf16[192,5120]{1,0:T(8,128)(2,1)}, bf16[192,5120]{1,0:T(8,128)(2,1)}, u32[]{:S(2)}, u32[]{:S(2)}) collective-permute-start(bf16[192,5120]{1,0:T(8,128)(2,1)} %get-tuple-element.49), channel_id=1, source_target_pairs={{0,2},{1,3},{2,0},{3,1},{4,6},{5,7},{6,4},{7,5}} | collective-permute-start | bytes 5898248 | tf_op jit(solution)/shard_map/ppermute | solution.py:240
  (6 other events, 230.3 us)

commit v2 on v1

v2 whole, which is shorter than its diff:
```python
import functools

import jax
import jax.numpy as jnp
from jax import lax
from jax.experimental import pallas as pl
from jax.experimental.pallas import tpu as pltpu
from jax.sharding import PartitionSpec as P


BF16 = jnp.bfloat16
F32 = jnp.float32
VMEM_LIMIT = 60 * 1024 * 1024
SPLIT = 1
DWD_BLOCK = 256
ANY = pl.BlockSpec(memory_space=pl.ANY)
NT = (((1,), (1,)), ((), ()))
TN = (((0,), (0,)), ((), ()))


def params():
    return pltpu.CompilerParams(vmem_limit_bytes=VMEM_LIMIT)


def cost(m, k, n, nbytes):
    return pl.CostEstimate(flops=2 * m * k * n, bytes_accessed=nbytes, transcendentals=0)


def gp_chunk(dys, wd, ug, uu, wg, wu, places):
    f, h = wd.shape
    total = sum(d.shape[0] for d in dys)
    shard = ug.shape[0] // 8
    half = total // 2
    bg, bp = 512, 512
    gsteps, psteps = f // bg, h // bp
    rest = f - gsteps * bg
    nd, npc = len(dys), len(places)
    part = total // SPLIT
    nk = 4
    kb = h // nk

    def kernel(*refs):
        dy_refs = refs[:nd]
        wd_ref, ug_ref, uu_ref, wg_ref, wu_ref = refs[nd : nd + 5]
        own_ref, oth_ref, dug_out, duu_out, zt_out = refs[nd + 5 : nd + 10]
        lhs, wdb, ugs, uus, du, zt, gs, wbuf, lsem, dsem, ksem, usem, osem, wsem = refs[nd + 10 :]
        i = pl.program_id(0)
        me = lax.axis_index("tp")

        def lhs_copies(k):
            off, out = 0, []
            cols = pl.ds(k * kb, kb)
            for j, d in enumerate(dy_refs):
                out.append(pltpu.make_async_copy(d.at[:, cols], lhs.at[pl.ds(off, d.shape[0]), cols], lsem.at[k, j]))
                off += d.shape[0]
            out.append(pltpu.make_async_copy(wd_ref.at[pl.ds(0, bg), cols], wdb.at[0, :, cols], ksem.at[k]))
            return out

        def wd_copy(b):
            n = bg if b < gsteps else rest
            return pltpu.make_async_copy(
                wd_ref.at[pl.ds(b * bg, n), :], wdb.at[b % 2, pl.ds(0, n), :], dsem.at[b]
            )

        def u_copies(b):
            off, out = 0, []
            cols = pl.ds(b * bg, bg if b < gsteps else rest)
            for j, (mask, first, rows) in enumerate(places):
                src = pl.ds(pl.multiple_of(jnp.bitwise_xor(me, mask) * shard + first, 64), rows)
                for k, (a, s) in enumerate(((ug_ref, ugs), (uu_ref, uus))):
                    out.append(
                        pltpu.make_async_copy(a.at[src, cols], s.at[pl.ds(off, rows), cols], usem.at[b, k, j])
                    )
                off += rows
            return out

        def out_copy(k):
            src = (du.at[:, pl.ds(0, f)], du.at[:, pl.ds(f, f)], zt)[k]
            return pltpu.make_async_copy(src, (dug_out, duu_out, zt_out)[k], osem.at[k])

        def w_copies(step, slot):
            rows = pl.ds(pl.multiple_of(step * bp, bp), bp)
            return [
                pltpu.make_async_copy(w.at[rows, :], wbuf.at[slot, :, pl.ds(k * f, f)], wsem.at[slot, k])
                for k, w in enumerate((wg_ref, wu_ref))
            ]

        def start(copies):
            for c in copies:
                c.start()

        def wait(copies):
            for c in copies:
                c.wait()

        def epilogue(col, wide, first, rows):
            cols = pl.ds(pl.multiple_of(col, 256), wide)
            cols2 = pl.ds(pl.multiple_of(col + f, 256), wide)
            for q in range(0, rows, 128):
                r = pl.ds(pl.multiple_of(first + q, 128), 128)
                a32 = ugs[r, cols].astype(F32)
                u32 = uus[r, cols].astype(F32)
                s = 0.5 * jnp.tanh(0.5 * a32) + 0.5
                act = a32 * s
                g = gs[r, pl.ds(0, wide)]
                du[r, cols] = (g * (u32 * s * (1.0 + a32 * (1.0 - s)))).astype(BF16)
                du[r, cols2] = (g * act).astype(BF16)
                zt[cols, r] = (act * u32).astype(BF16).T

        @pl.when(i == 0)
        def _():
            for k in range(nk):
                start(lhs_copies(k))
            start([wd_copy(1)] + u_copies(0))

            def quarter(k, carry):
                for j in range(nk):

                    @pl.when(k == j)
                    def _():
                        wait(lhs_copies(j))

                cols = pl.ds(pl.multiple_of(k * kb, kb), kb)
                g = lax.dot_general(lhs[:, cols], wdb[0, :, cols], NT, preferred_element_type=F32)
                gs[...] = gs[...] + g
                return carry

            gs[...] = jnp.zeros_like(gs)
            lax.fori_loop(0, nk, quarter, 0)

        for b in range(1, gsteps):

            @pl.when(i == b)
            def _():
                start([wd_copy(b + 1)] + u_copies(b))
                wait([wd_copy(b)] + u_copies(b - 1))

        @pl.when((i > 0) & (i < gsteps))
        def _():
            def rows_of(j, carry):
                first = pl.multiple_of(j * part, 128)
                epilogue((i - 1) * bg, bg, first, part)
                r = pl.ds(first, part)
                gs[r, :] = lax.dot_general(lhs[r, :], wdb[lax.rem(i, 2)], NT, preferred_element_type=F32)
                return carry

            if SPLIT == 1:
                rows_of(0, 0)
            else:
                lax.fori_loop(0, SPLIT, rows_of, 0)

        @pl.when(i == gsteps)
        def _():
            start(u_copies(gsteps) + w_copies(0, 0) + w_copies(1, 1))
            wait([wd_copy(gsteps)] + u_copies(gsteps - 1))
            epilogue((gsteps - 1) * bg, bg, 0, total)
            gs[:, pl.ds(0, rest)] = lax.dot_general(
                lhs[...], wdb[gsteps % 2, pl.ds(0, rest), :], NT, preferred_element_type=F32
            )
            wait(u_copies(gsteps))

            def rows_of(j, carry):
                epilogue(gsteps * bg, rest, j * 128, 128)
                return carry

            lax.fori_loop(0, total // 128, rows_of, 0)

        @pl.when(i > gsteps)
        def _():
            step = i - gsteps - 1
            slot = lax.rem(step, 2)

            @pl.when((step > 0) & (step + 1 < psteps))
            def _():
                start(w_copies(step + 1, 1 - slot))

            for k in range(3):

                @pl.when(step == k + 1)
                def _():
                    out_copy(k).start()

            wait(w_copies(step, slot))
            acc = lax.dot_general(du[...], wbuf[slot], NT, preferred_element_type=F32)
            own_ref[...] = acc[:half].astype(BF16)
            oth_ref[...] = acc[half:].astype(BF16)

        @pl.when(i == gsteps + psteps)
        def _():
            wait([out_copy(k) for k in range(3)])

    p_block = lambda i: jnp.maximum(i - gsteps - 1, 0)
    return pl.pallas_call(
        kernel,
        grid=(gsteps + 1 + psteps,),
        in_specs=[ANY] * (nd + 5),
        out_specs=[pl.BlockSpec((half, bp), lambda i: (0, p_block(i)))] * 2 + [ANY] * 3,
        scratch_shapes=[
            pltpu.VMEM((total, h), BF16),
            pltpu.VMEM((2, bg, h), BF16),
            pltpu.VMEM((total, f), BF16),
            pltpu.VMEM((total, f), BF16),
            pltpu.VMEM((total, 2 * f), BF16),
            pltpu.VMEM((f, total), BF16),
            pltpu.VMEM((total, bg), F32),
            pltpu.VMEM((2, bp, 2 * f), BF16),
            pltpu.SemaphoreType.DMA((nk, nd)),
            pltpu.SemaphoreType.DMA((gsteps + 1,)),
            pltpu.SemaphoreType.DMA((nk,)),
            pltpu.SemaphoreType.DMA((gsteps + 1, 2, npc)),
            pltpu.SemaphoreType.DMA((3,)),
            pltpu.SemaphoreType.DMA((2, 2)),
        ],
        out_shape=[
            jax.ShapeDtypeStruct((half, h), BF16),
            jax.ShapeDtypeStruct((half, h), BF16),
            jax.ShapeDtypeStruct((total, f), BF16),
            jax.ShapeDtypeStruct((total, f), BF16),
            jax.ShapeDtypeStruct((f, total), BF16),
        ],
        compiler_params=params(),
        cost_estimate=cost(total, 3 * h, f, 2 * (3 * f * h + total * (2 * h + 5 * f))),
        name="gp_chunk",
    )(*dys, wd, ug, uu, wg, wu)


def dw(streamed, moves, resident, transposed, bn):
    ns, nm, nc = len(streamed), len(moves), len(resident[0])
    nr = len(resident) * nc
    h = streamed[0].shape[1]
    if transposed:
        rows, f = resident[0][0].shape
        res_shape = (rows * nc, len(resident) * f)
        out_block, out_map, out_shape = (bn, f), lambda i: (i, 0), (h, f)
    else:
        f, rows = resident[0][0].shape
        res_shape = (f, rows * nc)
        out_block, out_map, out_shape = (f, bn), lambda i: (0, i), (f, h)
    tokens, nout = rows * nc, len(resident)
    steps = h // bn

    def kernel(*refs):
        s_refs = refs[:ns]
        r_refs = refs[ns : ns + nr]
        outs = refs[ns + nr : ns + nr + nout]
        buf, res, sem, rsem = refs[ns + nr + nout :]
        i = pl.program_id(0)
        slot = lax.rem(i, 2)

        def block(step, where):
            cols = pl.ds(pl.multiple_of(step * bn, bn), bn)
            return [
                pltpu.make_async_copy(
                    s_refs[a].at[pl.ds(src, n), cols], buf.at[where, pl.ds(dst, n), :], sem.at[where, m]
                )
                for m, (a, src, n, dst) in enumerate(moves)
            ]

        def chunk(c):
            out = []
            for k in range(nout):
                toks = pl.ds(c * rows, rows)
                dst = res.at[toks, pl.ds(k * f, f)] if transposed else res.at[:, toks]
                out.append(pltpu.make_async_copy(r_refs[k * nc + c], dst, rsem.at[k, c]))
            return out

        def dot(where, toks):
            s = buf[where, toks, :]
            if transposed:
                return lax.dot_general(s, res[toks, :], TN, preferred_element_type=F32)
            return jnp.dot(res[:, toks], s, preferred_element_type=F32)

        @pl.when(i == 0)
        def _():
            for c in block(0, 0):
                c.start()
            for c in range(nc):
                for d in chunk(c):
                    d.start()

        @pl.when(i + 1 < steps)
        def _():
            for c in block(i + 1, 1 - slot):
                c.start()

        for c in block(i, slot):
            c.wait()

        @pl.when(i == 0)
        def _():
            for o in outs:
                o[...] = jnp.zeros_like(o)

            def add_chunk(c, carry):
                for j in range(nc):

                    @pl.when(c == j)
                    def _():
                        for d in chunk(j):
                            d.wait()

                toks = pl.ds(pl.multiple_of(c * rows, rows), rows)
                p = dot(0, toks)
                for k, o in enumerate(outs):
                    o[...] += p[:, k * f : (k + 1) * f] if transposed else p
                return carry

            lax.fori_loop(0, nc, add_chunk, 0)

        @pl.when(i > 0)
        def _():
            p = dot(slot, pl.ds(0, tokens))
            for k, o in enumerate(outs):
                o[...] = p[:, k * f : (k + 1) * f] if transposed else p

    return pl.pallas_call(
        kernel,
        grid=(steps,),
        in_specs=[ANY] * (ns + nr),
        out_specs=[pl.BlockSpec(out_block, out_map)] * nout,
        out_shape=[jax.ShapeDtypeStruct(out_shape, F32)] * nout,
        scratch_shapes=[
            pltpu.VMEM((2, tokens, bn), BF16),
            pltpu.VMEM(res_shape, BF16),
            pltpu.SemaphoreType.DMA((2, nm)),
            pltpu.SemaphoreType.DMA((nout, nc)),
        ],
        compiler_params=params(),
        cost_estimate=cost(tokens, h, nout * f, 2 * tokens * (h + nout * f) + 4 * nout * h * f),
        name="dw",
    )(*streamed, *[r for group in resident for r in group])


def dx_sum(base, rx, ry):
    t, h = base.shape
    bc = h // 2
    u = t // 2

    def kernel(base_ref, rx0, rx1, ry0, ry1, out_ref):
        for k, (a, b) in enumerate(((rx0, ry0), (rx1, ry1))):

            @pl.when(pl.program_id(0) == k)
            def _():
                total = base_ref[...].astype(F32) + a[...].astype(F32) + b[...].astype(F32)
                out_ref[...] = total.astype(BF16)

    first = pl.BlockSpec((u, bc), lambda i, j: (0, jnp.where(i == 0, j, 1)))
    second = pl.BlockSpec((u, bc), lambda i, j: (0, jnp.where(i == 1, j, 0)))
    both = pl.BlockSpec((u, bc), lambda i, j: (i, j))
    return pl.pallas_call(
        kernel,
        grid=(2, 2),
        in_specs=[both, first, second, first, second],
        out_specs=both,
        out_shape=jax.ShapeDtypeStruct((t, h), BF16),
        compiler_params=params(),
        cost_estimate=cost(t, 2, h, 8 * t * h),
        name="dx_sum",
    )(base, *rx, *ry)


def solution(mesh):
    tok = P(("dp", "tp"), None)
    col = P(None, "tp")
    row = P("tp", None)
    act = P("dp", "tp")
    n = mesh.shape["tp"]
    pairs = {m: [(i, i ^ m) for i in range(n)] for m in (1, 2, 4)}
    core, xn, yn = pairs[1], pairs[2], pairs[4]

    def send(a, to):
        return lax.ppermute(a, "tp", to)

    def add(*terms):
        return functools.reduce(lambda a, b: a + b, [t.astype(F32) for t in terms]).astype(BF16)

    def inner(x, dy, wg, wu, wd, ug, uu):
        t = x.shape[0]
        u = t // 2
        dyp = [dy[:u], dy[u:]]
        dyc = send(dy, core)
        dyx0 = send(dyp[0], xn)
        dyy1 = send(dyp[1], yn)
        dyx1 = send(dyp[1], xn)
        dyy0 = send(dyp[0], yn)
        dyxc0, dyyc1 = send(dyx0, core), send(dyy1, core)
        dyd0, dyd1 = send(dyx0, yn), send(dyy1, xn)
        dyxc1, dyyc0 = send(dyx1, core), send(dyy0, core)
        dydc0, dydc1 = send(dyd0, core), send(dyd1, core)
        xp = [x[:u], x[u:]]
        xc = send(x, core)
        xx0, xy1 = send(xp[0], xn), send(xp[1], yn)
        xx1, xy0 = send(xp[1], xn), send(xp[0], yn)
        xd0, xd1 = send(xx0, yn), send(xy1, xn)
        xxc0, xyc1 = send(xx0, core), send(xy1, core)
        xxc1, xyc0 = send(xx1, core), send(xy0, core)
        xdc0, xdc1 = send(xd0, core), send(xd1, core)

        chunks = (
            ([dy, dyc], [(0, 0, t), (1, 0, t)]),
            ([dyx0, dyy1, dyxc0, dyyc1], [(2, 0, u), (4, u, u), (3, 0, u), (5, u, u)]),
            ([dyx1, dyy0, dyxc1, dyyc0], [(2, u, u), (4, 0, u), (3, u, u), (5, 0, u)]),
            ([dyd0, dyd1, dydc0, dydc1], [(6, 0, t), (7, 0, t)]),
        )
        own, oth, dug, duu, zt = [], [], [], [], []
        for rows, places in chunks:
            res = gp_chunk(rows, wd, ug, uu, wg, wu, places)
            for dst, r in zip((own, oth, dug, duu, zt), res):
                dst.append(r)
        got = [send(oth[c], core) for c in range(4)]
        mine = lambda c, j: (own[c][j * u : (j + 1) * u], got[c][j * u : (j + 1) * u])
        rdx = send(add(*mine(3, 0)), xn)
        rdy = send(add(*mine(3, 1)), yn)
        qx0, qy1 = add(*mine(1, 0)), add(*mine(1, 1))
        rx0, ry1 = send(qx0, xn), send(qy1, yn)
        rx1 = send(add(*mine(2, 0), rdy), xn)
        ry0 = send(add(*mine(2, 1), rdx), yn)
        base = add(own[0], got[0])
        dx = dx_sum(base, (rx0, rx1), (ry0, ry1))

        def moves(parts):
            out, dst = [], 0
            for a, src, rows in parts:
                out.append((a, src, rows, dst))
                dst += rows
            return out

        dy_arrays = [a for rows, _ in chunks for a in rows]
        dy_moves = moves([(k, 0, a.shape[0]) for k, a in enumerate(dy_arrays)])
        (dwd,) = dw(dy_arrays, dy_moves, [zt], False, DWD_BLOCK)
        x_arrays = [x, xc, xx0, xy1, xxc0, xyc1, xx1, xy0, xxc1, xyc0, xd0, xd1, xdc0, xdc1]
        x_moves = moves([(k, 0, a.shape[0]) for k, a in enumerate(x_arrays)])
        dwg, dwu = dw(x_arrays, x_moves, [dug, duu], True, 256)
        return dx, dwg, dwu, dwd

    return jax.shard_map(
        inner, mesh=mesh, in_specs=(tok, tok, col, col, row, act, act), out_specs=(tok, act, act, tok), check_vma=False
    )
```

time: 621 us -> 633 us (1.019)
  waiting for transfers between devices: 120 us -> 149 us
  Pallas kernels: 441 us -> 419 us
    ppermute x32 -> x36, waiting for transfers between devices: 120 us -> 149 us  [send(): return lax.ppermute(a, 'tp', to)]
    pallas_call x4 -> x5, Pallas kernels: 240 us -> 226 us  [the longest x4 219 us: gp_chunk(): pl.pallas_call(kernel, grid=(gsteps + 1 + psteps,), in_specs=[ANY] * (nd...]
    pallas_call x3 -> x2, Pallas kernels: 202 us -> 193 us  [dw(): pl.pallas_call(kernel, grid=(steps,), in_specs=[ANY] * (ns + nr), out_spe...]
    ppermute x32 -> x36, starting transfers between devices: 21.6 us -> 26.3 us  [send(): return lax.ppermute(a, 'tp', to)]
  transfers between devices with their start and end apart: 32 -> 36, of which waited for: 3 -> 6; matrix products, arithmetic and copies ran while one was open for 4% -> 4% of each run, Pallas kernels for 72% -> 66%
where the time goes in v2:
time: 633 us; the launch traced here: 626 us
  Pallas kernels  419 us (66%)
  waiting for transfers between devices  149 us (24%)
  starting transfers between devices  26.3 us (4%)
  other arithmetic  23.5 us (4%)
  local copies, waits for them, and re-layouts  7.3 us (1%)
    pallas_call x4, Pallas kernels, gp_chunk(): pl.pallas_call(kernel, grid=(gsteps + 1 + psteps,), in_specs=[ANY] * (nd...  219 us
    pallas_call x2, Pallas kernels, dw(): pl.pallas_call(kernel, grid=(steps,), in_specs=[ANY] * (ns + nr), out_spe...  193 us
    ppermute x36, waiting for transfers between devices, send(): return lax.ppermute(a, 'tp', to)  149 us
    ppermute x36, starting transfers between devices, send(): return lax.ppermute(a, 'tp', to)  26.3 us
    convert_element_type x4, other arithmetic, add(): functools.reduce(lambda a, b: a + b, [t.astype(F32) for t in terms])  23.5 us
  transfers between devices with their start and end apart: 36, of which 6 were waited for; matrix products, arithmetic and copies ran while one was open for 4% of the time, Pallas kernels for 66%

profile of v2, /device:TPU:0, one launch (start us, length us, event | category | flops | bytes accessed | tf_op | source)
XLA Modules:
  0.0 626.3 jit_solution(7956993837826810149)
XLA Ops:
  0.7 3.8 fusion.1
  4.5 3.3 collective-permute-start.3
  7.8 1.5 collective-permute-start.2
  9.3 1.5 fusion
  10.8 0.5 collective-permute-start.28
  11.4 1.5 collective-permute-start.25
  12.9 38.9 %collective-permute-done.3.refs_1_.refs_3_ = bf16[192,5120]{1,0:T(8,128)(2,1)} collective-permute-done((bf16[192,5120]{1,0:T(8,128)(2,1)}, bf16[192,5120]{1,0:T(8,128)(2,1)}, u32[]{:S(2)}, u32[]{:S(2)}) %collective-permute-start.3) | collective-permute-done | bytes 1966112 | tf_op jit(solution)/shard_map/ppermute | solution.py:372
  51.8 2.0 collective-permute-start.14
  53.8 1.5 collective-permute-start.13
  55.3 40.3 %collective-permute-done.28.refs_6_ = bf16[192,5120]{1,0:T(8,128)(2,1)S(1)} collective-permute-done((bf16[192,5120]{1,0:T(8,128)(2,1)S(1)}, bf16[192,5120]{1,0:T(8,128)(2,1)S(1)}, u32[]{:S(2)}, u32[]{:S(2)}) %collective-permute-start.28) | collective-permute-done | bytes 1966112 | tf_op jit(solution)/shard_map/ppermute | solution.py:372
  95.7 2.0 collective-permute-start.24
  97.6 40.2 %collective-permute-done.14.refs_1_.refs_11_ = bf16[192,5120]{1,0:T(8,128)(2,1)} collective-permute-done((bf16[192,5120]{1,0:T(8,128)(2,1)}, bf16[192,5120]{1,0:T(8,128)(2,1)}, u32[]{:S(2)}, u32[]{:S(2)}) %collective-permute-start.14) | collective-permute-done | bytes 1966112 | tf_op jit(solution)/shard_map/ppermute | solution.py:372
  137.9 1.5 collective-permute-start.8
  139.4 1.9 copy-done.6
  141.8 53.8 %gp_chunk.4 = (bf16[384,5120]{1,0:T(8,128)(2,1)}, bf16[384,5120]{1,0:T(8,128)(2,1)}, bf16[768,1792]{1,0:T(8,128)(2,1)}, bf16[768,1792]{1,0:T(8,128)(2,1)}, bf16[1792,768]{1,0:T(8,128)(2,1)}) custom-call(bf16[384,5120]{1,0:T(8,128)(2,1)} %refs_0_.5, bf16[384,5120]{1,0:T(8,128)(2,1)} %copy-done.6, bf16[1792,5120]{1,0:T(8,128)(2,1)} %refs_4_.7, ...), custom_call_target="tpu_custom_call" | custom-call | flops 42278584320 | bytes 84541440 | tf_op jit(solution)/shard_map/gp_chunk/pallas_call | solution.py:193
  196.1 24.6 %collective-permute-done.8.refs_0_.refs_6_ = bf16[192,5120]{1,0:T(8,128)(2,1)} collective-permute-done((bf16[192,5120]{1,0:T(8,128)(2,1)}, bf16[192,5120]{1,0:T(8,128)(2,1)}, u32[]{:S(2)}, u32[]{:S(2)}) %collective-permute-start.8) | collective-permute-done | bytes 1966112 | tf_op jit(solution)/shard_map/ppermute | solution.py:372
  221.2 1.5 collective-permute-start.33
  222.7 54.6 %gp_chunk.7 = (bf16[384,5120]{1,0:T(8,128)(2,1)}, bf16[384,5120]{1,0:T(8,128)(2,1)}, bf16[768,1792]{1,0:T(8,128)(2,1)}, bf16[768,1792]{1,0:T(8,128)(2,1)}, bf16[1792,768]{1,0:T(8,128)(2,1)}) custom-call(bf16[192,5120]{1,0:T(8,128)(2,1)} %collective-permute-done.13.refs_0_.refs_10_, bf16[192,5120]{1,0:T(8,128)(2,1)} %collective-permute-done.14.refs_1_.refs_11_, ...), custom_call_target="tpu_custom_call" | custom-call | flops 42278584320 | bytes 84541440 | tf_op jit(solution)/shard_map/gp_chunk/pallas_call | solution.py:193
  278.6 55.3 %gp_chunk.5 = (bf16[384,5120]{1,0:T(8,128)(2,1)}, bf16[384,5120]{1,0:T(8,128)(2,1)}, bf16[768,1792]{1,0:T(8,128)(2,1)}, bf16[768,1792]{1,0:T(8,128)(2,1)}, bf16[1792,768]{1,0:T(8,128)(2,1)}) custom-call(bf16[192,5120]{1,0:T(8,128)(2,1)} %copy-done.7, bf16[192,5120]{1,0:T(8,128)(2,1)} %collective-permute-done.3.refs_1_.refs_3_, ...), custom_call_target="tpu_custom_call" | custom-call | flops 42278584320 | bytes 84541440 | tf_op jit(solution)/shard_map/gp_chunk/pallas_call | solution.py:193
  335.3 55.5 %gp_chunk.6 = (bf16[384,5120]{1,0:T(8,128)(2,1)}, bf16[384,5120]{1,0:T(8,128)(2,1)}, bf16[768,1792]{1,0:T(8,128)(2,1)}, bf16[768,1792]{1,0:T(8,128)(2,1)}, bf16[1792,768]{1,0:T(8,128)(2,1)}) custom-call(bf16[192,5120]{1,0:T(8,128)(2,1)} %collective-permute-done.8.refs_0_.refs_6_, bf16[192,5120]{1,0:T(8,128)(2,1)} %collective-permute-done.9.refs_1_.refs_7_, ...), custom_call_target="tpu_custom_call" | custom-call | flops 42278584320 | bytes 84541440 | tf_op jit(solution)/shard_map/gp_chunk/pallas_call | solution.py:193
  390.8 6.7 %add_convert_fusion.3 = (bf16[192,5120]{1,0:T(8,128)(2,1)}, bf16[192,5120]{1,0:T(8,128)(2,1)}) fusion(bf16[384,5120]{1,0:T(8,128)(2,1)} %collective-permute-done.17, bf16[384,5120]{1,0:T(8,128)(2,1)} %get-tuple-element.32), kind=kLoop, calls=%fused_computation.3 | loop fusion | flops 7864320 | bytes 11796480 | tf_op jit(solution)/shard_map/convert_element_type | solution.py:375
  398.5 1.7 collective-permute-start.18
  400.2 125.7 %dw.2 = (f32[5120,1792]{1,0:T(8,128)}, f32[5120,1792]{1,0:T(8,128)}) custom-call(bf16[384,5120]{1,0:T(8,128)(2,1)} %refs_0_.4, bf16[384,5120]{1,0:T(8,128)(2,1)} %collective-permute-done.23.refs_1_, bf16[192,5120]{1,0:T(8,128)(2,1)} %collective-permute-done.24.refs_2_, bf16[192,5120]{1,0:T(8,128)(2,1)} %copy-done.9, ...), custom_call_target="tpu_custom_call" | custom-call | flops 112742891520 | bytes 126877696 | tf_op jit(solution)/shard_map/dw/pallas_call | solution.py:316
  526.0 5.7 add_convert_fusion.1
  532.0 1.7 collective-permute-start.7
  533.7 5.5 add_convert_fusion.2
  539.3 1.5 collective-permute-start.21
  540.8 0.5 collective-permute-start.19
  541.3 67.3 %dw.3 = f32[1792,5120]{1,0:T(8,128)} custom-call(bf16[384,5120]{1,0:T(8,128)(2,1)} %refs_0_.5, bf16[384,5120]{1,0:T(8,128)(2,1)} %copy-done.6, bf16[192,5120]{1,0:T(8,128)(2,1)} %copy-done.7, bf16[192,5120]{1,0:T(8,128)(2,1)} %collective-permute-done.3.refs_1_.refs_3_, bf16[192,5120]{1,0:T(8,128)(2,1)} %collective-permute-done.4.refs_2_.refs_4_, ...), custom_call_target="tpu_custom_call" | custom-call | flops 56371445760 | bytes 79167488 | tf_op jit(solution)/shard_map/dw/pallas_call | solution.py:316
  608.7 5.5 add_convert_fusion.base_ref
  614.2 4.5 collective-permute-done.21.ry0
  618.8 7.3 %dx_sum.1 = bf16[384,5120]{1,0:T(8,128)(2,1)} custom-call(bf16[384,5120]{1,0:T(8,128)(2,1)} %add_convert_fusion.base_ref, bf16[192,5120]{1,0:T(8,128)(2,1)} %collective-permute-done.7.rx0, bf16[192,5120]{1,0:T(8,128)(2,1)} %collective-permute-done.19.rx1, bf16[192,5120]{1,0:T(8,128)(2,1)} %collective-permute-done.21.ry0, ...), custom_call_target="tpu_custom_call" | custom-call | flops 7864320 | bytes 15728640 | tf_op jit(solution)/shard_map/dx_sum/pallas_call | solution.py:350
  (73 shorter events, 5.7 us)
Async XLA Ops:
  9.3 130.1 %collective-permute-start = (bf16[384,5120]{1,0:T(8,128)(2,1)S(1)}, bf16[384,5120]{1,0:T(8,128)(2,1)S(1)}, u32[]{:S(2)}, u32[]{:S(2)}) collective-permute-start(bf16[384,5120]{1,0:T(8,128)(2,1)S(1)} %copy-done.1), channel_id=1, source_target_pairs={{0,1},{1,0},{2,3},{3,2},{4,5},{5,4},{6,7},{7,6}} | collective-permute-start | bytes 11796488 | tf_op jit(solution)/shard_map/ppermute | solution.py:372
  10.8 84.8 %collective-permute-start.28 = (bf16[192,5120]{1,0:T(8,128)(2,1)S(1)}, bf16[192,5120]{1,0:T(8,128)(2,1)S(1)}, u32[]{:S(2)}, u32[]{:S(2)}) collective-permute-start(bf16[192,5120]{1,0:T(8,128)(2,1)S(1)} %get-tuple-element.54), channel_id=1, source_target_pairs={{0,2},{1,3},{2,0},{3,1},{4,6},{5,7},{6,4},{7,5}} | collective-permute-start | bytes 5898248 | tf_op jit(solution)/shard_map/ppermute | solution.py:372
  11.4 84.3 %collective-permute-start.25 = (bf16[192,5120]{1,0:T(8,128)(2,1)S(1)}, bf16[192,5120]{1,0:T(8,128)(2,1)S(1)}, u32[]{:S(2)}, u32[]{:S(2)}) collective-permute-start(bf16[192,5120]{1,0:T(8,128)(2,1)S(1)} %get-tuple-element.54), channel_id=1, source_target_pairs={{0,4},{1,5},{2,6},{3,7},{4,0},{5,1},{6,2},{7,3}} | collective-permute-start | bytes 5898248 | tf_op jit(solution)/shard_map/ppermute | solution.py:372
  51.8 86.1 %collective-permute-start.14 = (bf16[192,5120]{1,0:T(8,128)(2,1)}, bf16[192,5120]{1,0:T(8,128)(2,1)}, u32[]{:S(2)}, u32[]{:S(2)}) collective-permute-start(bf16[192,5120]{1,0:T(8,128)(2,1)} %collective-permute-done.3.refs_1_.refs_3_), channel_id=1, source_target_pairs={{0,2},{1,3},{2,0},{3,1},{4,6},{5,7},{6,4},{7,5}} | collective-permute-start | bytes 5898248 | tf_op jit(solution)/shard_map/ppermute | solution.py:372
  53.8 85.6 %collective-permute-start.13 = (bf16[192,5120]{1,0:T(8,128)(2,1)S(1)}, bf16[192,5120]{1,0:T(8,128)(2,1)}, u32[]{:S(2)}, u32[]{:S(2)}) collective-permute-start(bf16[192,5120]{1,0:T(8,128)(2,1)S(1)} %collective-permute-done.2.refs_0_.refs_2_), channel_id=1, source_target_pairs={{0,4},{1,5},{2,6},{3,7},{4,0},{5,1},{6,2},{7,3}} | collective-permute-start | bytes 5898248 | tf_op jit(solution)/shard_map/ppermute | solution.py:372
  95.6 100.0 %collective-permute-start.29 = (bf16[192,5120]{1,0:T(8,128)(2,1)}, bf16[192,5120]{1,0:T(8,128)(2,1)}, u32[]{:S(2)}, u32[]{:S(2)}) collective-permute-start(bf16[192,5120]{1,0:T(8,128)(2,1)} %get-tuple-element.55), channel_id=1, source_target_pairs={{0,4},{1,5},{2,6},{3,7},{4,0},{5,1},{6,2},{7,3}} | collective-permute-start | bytes 5898248 | tf_op jit(solution)/shard_map/ppermute | solution.py:372
  95.7 100.5 %collective-permute-start.24 = (bf16[192,5120]{1,0:T(8,128)(2,1)}, bf16[192,5120]{1,0:T(8,128)(2,1)}, u32[]{:S(2)}, u32[]{:S(2)}) collective-permute-start(bf16[192,5120]{1,0:T(8,128)(2,1)} %get-tuple-element.55), channel_id=1, source_target_pairs={{0,2},{1,3},{2,0},{3,1},{4,6},{5,7},{6,4},{7,5}} | collective-permute-start | bytes 5898248 | tf_op jit(solution)/shard_map/ppermute | solution.py:372
  137.9 82.9 %collective-permute-start.8 = (bf16[192,5120]{1,0:T(8,128)(2,1)}, bf16[192,5120]{1,0:T(8,128)(2,1)}, u32[]{:S(2)}, u32[]{:S(2)}) collective-permute-start(bf16[192,5120]{1,0:T(8,128)(2,1)} %get-tuple-element.56), channel_id=1, source_target_pairs={{0,2},{1,3},{2,0},{3,1},{4,6},{5,7},{6,4},{7,5}} | collective-permute-start | bytes 5898248 | tf_op jit(solution)/shard_map/ppermute | solution.py:372
  139.4 81.4 %collective-permute-start.16 = (bf16[192,5120]{1,0:T(8,128)(2,1)}, bf16[192,5120]{1,0:T(8,128)(2,1)}, u32[]{:S(2)}, u32[]{:S(2)}) collective-permute-start(bf16[192,5120]{1,0:T(8,128)(2,1)} %collective-permute-done.14.refs_1_.refs_11_), channel_id=1, source_target_pairs={{0,1},{1,0},{2,3},{3,2},{4,5},{5,4},{6,7},{7,6}} | collective-permute-start | bytes 5898248 | tf_op jit(solution)/shard_map/ppermute | solution.py:372
  141.3 79.9 %collective-permute-start.15 = (bf16[192,5120]{1,0:T(8,128)(2,1)}, bf16[192,5120]{1,0:T(8,128)(2,1)}, u32[]{:S(2)}, u32[]{:S(2)}) collective-permute-start(bf16[192,5120]{1,0:T(8,128)(2,1)} %collective-permute-done.13.refs_0_.refs_10_), channel_id=1, source_target_pairs={{0,1},{1,0},{2,3},{3,2},{4,5},{5,4},{6,7},{7,6}} | collective-permute-start | bytes 5898248 | tf_op jit(solution)/shard_map/ppermute | solution.py:372
  195.6 81.7 %collective-permute-start.9 = (bf16[192,5120]{1,0:T(8,128)(2,1)}, bf16[192,5120]{1,0:T(8,128)(2,1)}, u32[]{:S(2)}, u32[]{:S(2)}) collective-permute-start(bf16[192,5120]{1,0:T(8,128)(2,1)} %copy-done.5), channel_id=1, source_target_pairs={{0,4},{1,5},{2,6},{3,7},{4,0},{5,1},{6,2},{7,3}} | collective-permute-start | bytes 5898248 | tf_op jit(solution)/shard_map/ppermute | solution.py:372
  196.1 82.0 %collective-permute-start.5 = (bf16[192,5120]{1,0:T(8,128)(2,1)}, bf16[192,5120]{1,0:T(8,128)(2,1)}, u32[]{:S(2)}, u32[]{:S(2)}) collective-permute-start(bf16[192,5120]{1,0:T(8,128)(2,1)} %collective-permute-done.3.refs_1_.refs_3_), channel_id=1, source_target_pairs={{0,1},{1,0},{2,3},{3,2},{4,5},{5,4},{6,7},{7,6}} | collective-permute-start | bytes 5898248 | tf_op jit(solution)/shard_map/ppermute | solution.py:372
  220.7 57.7 %collective-permute-start.4 = (bf16[192,5120]{1,0:T(8,128)(2,1)}, bf16[192,5120]{1,0:T(8,128)(2,1)}, u32[]{:S(2)}, u32[]{:S(2)}) collective-permute-start(bf16[192,5120]{1,0:T(8,128)(2,1)} %copy-done.7), channel_id=1, source_target_pairs={{0,1},{1,0},{2,3},{3,2},{4,5},{5,4},{6,7},{7,6}} | collective-permute-start | bytes 5898248 | tf_op jit(solution)/shard_map/ppermute | solution.py:372
  220.7 56.7 %collective-permute-start.30 = (bf16[192,5120]{1,0:T(8,128)(2,1)}, bf16[192,5120]{1,0:T(8,128)(2,1)}, u32[]{:S(2)}, u32[]{:S(2)}) collective-permute-start(bf16[192,5120]{1,0:T(8,128)(2,1)} %copy-done.8), channel_id=1, source_target_pairs={{0,1},{1,0},{2,3},{3,2},{4,5},{5,4},{6,7},{7,6}} | collective-permute-start | bytes 5898248 | tf_op jit(solution)/shard_map/ppermute | solution.py:372
  221.2 56.7 %collective-permute-start.33 = (bf16[192,5120]{1,0:T(8,128)(2,1)}, bf16[192,5120]{1,0:T(8,128)(2,1)}, u32[]{:S(2)}, u32[]{:S(2)}) collective-permute-start(bf16[192,5120]{1,0:T(8,128)(2,1)} %copy-done.9), channel_id=1, source_target_pairs={{0,2},{1,3},{2,0},{3,1},{4,6},{5,7},{6,4},{7,5}} | collective-permute-start | bytes 5898248 | tf_op jit(solution)/shard_map/ppermute | solution.py:372
  277.4 56.5 %collective-permute-start.27 = (bf16[192,5120]{1,0:T(8,128)(2,1)}, bf16[192,5120]{1,0:T(8,128)(2,1)}, u32[]{:S(2)}, u32[]{:S(2)}) collective-permute-start(bf16[192,5120]{1,0:T(8,128)(2,1)} %copy-done.9), channel_id=1, source_target_pairs={{0,1},{1,0},{2,3},{3,2},{4,5},{5,4},{6,7},{7,6}} | collective-permute-start | bytes 5898248 | tf_op jit(solution)/shard_map/ppermute | solution.py:372
  277.4 56.9 %collective-permute-start.32 = (bf16[192,5120]{1,0:T(8,128)(2,1)}, bf16[192,5120]{1,0:T(8,128)(2,1)}, u32[]{:S(2)}, u32[]{:S(2)}) collective-permute-start(bf16[192,5120]{1,0:T(8,128)(2,1)} %collective-permute-done.24.refs_2_), channel_id=1, source_target_pairs={{0,4},{1,5},{2,6},{3,7},{4,0},{5,1},{6,2},{7,3}} | collective-permute-start | bytes 5898248 | tf_op jit(solution)/shard_map/ppermute | solution.py:372
  278.1 56.7 %collective-permute-start.11 = (bf16[192,5120]{1,0:T(8,128)(2,1)}, bf16[192,5120]{1,0:T(8,128)(2,1)}, u32[]{:S(2)}, u32[]{:S(2)}) collective-permute-start(bf16[192,5120]{1,0:T(8,128)(2,1)} %collective-permute-done.9.refs_1_.refs_7_), channel_id=1, source_target_pairs={{0,1},{1,0},{2,3},{3,2},{4,5},{5,4},{6,7},{7,6}} | collective-permute-start | bytes 5898248 | tf_op jit(solution)/shard_map/ppermute | solution.py:372
  333.9 64.1 %collective-permute-start.23 = (bf16[384,5120]{1,0:T(8,128)(2,1)S(1)}, bf16[384,5120]{1,0:T(8,128)(2,1)}, u32[]{:S(2)}, u32[]{:S(2)}) collective-permute-start(bf16[384,5120]{1,0:T(8,128)(2,1)S(1)} %copy-done), channel_id=1, source_target_pairs={{0,1},{1,0},{2,3},{3,2},{4,5},{5,4},{6,7},{7,6}} | collective-permute-start | bytes 11796488 | tf_op jit(solution)/shard_map/ppermute | solution.py:372
  334.3 63.4 %collective-permute-start.26 = (bf16[192,5120]{1,0:T(8,128)(2,1)}, bf16[192,5120]{1,0:T(8,128)(2,1)}, u32[]{:S(2)}, u32[]{:S(2)}) collective-permute-start(bf16[192,5120]{1,0:T(8,128)(2,1)} %collective-permute-done.24.refs_2_), channel_id=1, source_target_pairs={{0,1},{1,0},{2,3},{3,2},{4,5},{5,4},{6,7},{7,6}} | collective-permute-start | bytes 5898248 | tf_op jit(solution)/shard_map/ppermute | solution.py:372
  334.4 63.0 %collective-permute-start.31 = (bf16[192,5120]{1,0:T(8,128)(2,1)}, bf16[192,5120]{1,0:T(8,128)(2,1)}, u32[]{:S(2)}, u32[]{:S(2)}) collective-permute-start(bf16[192,5120]{1,0:T(8,128)(2,1)} %collective-permute-done.29.refs_7_), channel_id=1, source_target_pairs={{0,1},{1,0},{2,3},{3,2},{4,5},{5,4},{6,7},{7,6}} | collective-permute-start | bytes 5898248 | tf_op jit(solution)/shard_map/ppermute | solution.py:372
  334.8 63.4 %collective-permute-start.35 = (bf16[192,5120]{1,0:T(8,128)(2,1)}, bf16[192,5120]{1,0:T(8,128)(2,1)}, u32[]{:S(2)}, u32[]{:S(2)}) collective-permute-start(bf16[192,5120]{1,0:T(8,128)(2,1)} %collective-permute-done.33.refs_11_), channel_id=1, source_target_pairs={{0,1},{1,0},{2,3},{3,2},{4,5},{5,4},{6,7},{7,6}} | collective-permute-start | bytes 5898248 | tf_op jit(solution)/shard_map/ppermute | solution.py:372
  335.0 63.5 %collective-permute-start.34 = (bf16[192,5120]{1,0:T(8,128)(2,1)}, bf16[192,5120]{1,0:T(8,128)(2,1)}, u32[]{:S(2)}, u32[]{:S(2)}) collective-permute-start(bf16[192,5120]{1,0:T(8,128)(2,1)} %collective-permute-done.32.refs_10_), channel_id=1, source_target_pairs={{0,1},{1,0},{2,3},{3,2},{4,5},{5,4},{6,7},{7,6}} | collective-permute-start | bytes 5898248 | tf_op jit(solution)/shard_map/ppermute | solution.py:372
  397.5 211.2 %collective-permute-start.1 = (bf16[384,5120]{1,0:T(8,128)(2,1)}, bf16[384,5120]{1,0:T(8,128)(2,1)}, u32[]{:S(2)}, u32[]{:S(2)}) collective-permute-start(bf16[384,5120]{1,0:T(8,128)(2,1)} %get-tuple-element.27), channel_id=1, source_target_pairs={{0,1},{1,0},{2,3},{3,2},{4,5},{5,4},{6,7},{7,6}} | collective-permute-start | bytes 11796488 | tf_op jit(solution)/shard_map/ppermute | solution.py:372
  397.6 128.3 %collective-permute-start.6 = (bf16[384,5120]{1,0:T(8,128)(2,1)}, bf16[384,5120]{1,0:T(8,128)(2,1)}, u32[]{:S(2)}, u32[]{:S(2)}) collective-permute-start(bf16[384,5120]{1,0:T(8,128)(2,1)} %get-tuple-element.29), channel_id=1, source_target_pairs={{0,1},{1,0},{2,3},{3,2},{4,5},{5,4},{6,7},{7,6}} | collective-permute-start | bytes 11796488 | tf_op jit(solution)/shard_map/ppermute | solution.py:372
  398.0 134.0 %collective-permute-start.12 = (bf16[384,5120]{1,0:T(8,128)(2,1)}, bf16[384,5120]{1,0:T(8,128)(2,1)}, u32[]{:S(2)}, u32[]{:S(2)}) collective-permute-start(bf16[384,5120]{1,0:T(8,128)(2,1)} %get-tuple-element.31), channel_id=1, source_target_pairs={{0,1},{1,0},{2,3},{3,2},{4,5},{5,4},{6,7},{7,6}} | collective-permute-start | bytes 11796488 | tf_op jit(solution)/shard_map/ppermute | solution.py:372
  398.2 135.6 %collective-permute-start.20 = (bf16[192,5120]{1,0:T(8,128)(2,1)}, bf16[192,5120]{1,0:T(8,128)(2,1)}, u32[]{:S(2)}, u32[]{:S(2)}) collective-permute-start(bf16[192,5120]{1,0:T(8,128)(2,1)} %get-tuple-element.52), channel_id=1, source_target_pairs={{0,2},{1,3},{2,0},{3,1},{4,6},{5,7},{6,4},{7,5}} | collective-permute-start | bytes 5898248 | tf_op jit(solution)/shard_map/ppermute | solution.py:372
  398.5 135.2 %collective-permute-start.18 = (bf16[192,5120]{1,0:T(8,128)(2,1)}, bf16[192,5120]{1,0:T(8,128)(2,1)}, u32[]{:S(2)}, u32[]{:S(2)}) collective-permute-start(bf16[192,5120]{1,0:T(8,128)(2,1)} %get-tuple-element.53), channel_id=1, source_target_pairs={{0,4},{1,5},{2,6},{3,7},{4,0},{5,1},{6,2},{7,3}} | collective-permute-start | bytes 5898248 | tf_op jit(solution)/shard_map/ppermute | solution.py:372
  531.7 82.5 %collective-permute-start.22 = (bf16[192,5120]{1,0:T(8,128)(2,1)}, bf16[192,5120]{1,0:T(8,128)(2,1)}, u32[]{:S(2)}, u32[]{:S(2)}) collective-permute-start(bf16[192,5120]{1,0:T(8,128)(2,1)} %get-tuple-element.48), channel_id=1, source_target_pairs={{0,4},{1,5},{2,6},{3,7},{4,0},{5,1},{6,2},{7,3}} | collective-permute-start | bytes 5898248 | tf_op jit(solution)/shard_map/ppermute | solution.py:372
  532.0 82.2 %collective-permute-start.7 = (bf16[192,5120]{1,0:T(8,128)(2,1)}, bf16[192,5120]{1,0:T(8,128)(2,1)}, u32[]{:S(2)}, u32[]{:S(2)}) collective-permute-start(bf16[192,5120]{1,0:T(8,128)(2,1)} %get-tuple-element.49), channel_id=1, source_target_pairs={{0,2},{1,3},{2,0},{3,1},{4,6},{5,7},{6,4},{7,5}} | collective-permute-start | bytes 5898248 | tf_op jit(solution)/shard_map/ppermute | solution.py:372
  539.3 79.4 %collective-permute-start.21 = (bf16[192,5120]{1,0:T(8,128)(2,1)}, bf16[192,5120]{1,0:T(8,128)(2,1)}, u32[]{:S(2)}, u32[]{:S(2)}) collective-permute-start(bf16[192,5120]{1,0:T(8,128)(2,1)} %get-tuple-element.50), channel_id=1, source_target_pairs={{0,4},{1,5},{2,6},{3,7},{4,0},{5,1},{6,2},{7,3}} | collective-permute-start | bytes 5898248 | tf_op jit(solution)/shard_map/ppermute | solution.py:372
  540.8 78.0 %collective-permute-start.19 = (bf16[192,5120]{1,0:T(8,128)(2,1)}, bf16[192,5120]{1,0:T(8,128)(2,1)}, u32[]{:S(2)}, u32[]{:S(2)}) collective-permute-start(bf16[192,5120]{1,0:T(8,128)(2,1)} %get-tuple-element.51), channel_id=1, source_target_pairs={{0,2},{1,3},{2,0},{3,1},{4,6},{5,7},{6,4},{7,5}} | collective-permute-start | bytes 5898248 | tf_op jit(solution)/shard_map/ppermute | solution.py:372
  (14 other events, 734.5 us)

commit v3 on v2

--- a/solution.py
+++ b/solution.py
@@ -12,7 +12,7 @@
 F32 = jnp.float32
 VMEM_LIMIT = 60 * 1024 * 1024
 SPLIT = 1
-DWD_BLOCK = 256
+DWD_BLOCK = 512
 ANY = pl.BlockSpec(memory_space=pl.ANY)
 NT = (((1,), (1,)), ((), ()))
 TN = (((0,), (0,)), ((), ()))
@@ -26,7 +26,7 @@
     return pl.CostEstimate(flops=2 * m * k * n, bytes_accessed=nbytes, transcendentals=0)
 
 
-def gp_chunk(dys, wd, ug, uu, wg, wu, places):
+def gp_chunk(dys, wd, ug, uu, wg, wu, places, whole=None):
     f, h = wd.shape
     total = sum(d.shape[0] for d in dys)
     shard = ug.shape[0] // 8
@@ -38,12 +38,14 @@
     part = total // SPLIT
     nk = 4
     kb = h // nk
+    nw = 0 if whole is None else 1
 
     def kernel(*refs):
         dy_refs = refs[:nd]
         wd_ref, ug_ref, uu_ref, wg_ref, wu_ref = refs[nd : nd + 5]
-        own_ref, oth_ref, dug_out, duu_out, zt_out = refs[nd + 5 : nd + 10]
-        lhs, wdb, ugs, uus, du, zt, gs, wbuf, lsem, dsem, ksem, usem, osem, wsem = refs[nd + 10 :]
+        outs = refs[nd + 5 + nw :]
+        own_ref, oth_ref, dug_out, duu_out, zt_out = outs[:5]
+        lhs, wdb, ugs, uus, du, zt, gs, wbuf, lsem, dsem, ksem, usem, osem, wsem = outs[5 + 2 * nw : 19 + 2 * nw]
         i = pl.program_id(0)
         me = lax.axis_index("tp")
 
@@ -77,6 +79,14 @@
         def out_copy(k):
             src = (du.at[:, pl.ds(0, f)], du.at[:, pl.ds(f, f)], zt)[k]
             return pltpu.make_async_copy(src, (dug_out, duu_out, zt_out)[k], osem.at[k])
+
+        def half_in(k):
+            r = pl.ds(k * (whole.shape[0] // 2), whole.shape[0] // 2)
+            return pltpu.make_async_copy(refs[nd + 5].at[r, :], outs[-2].at[r, :], outs[-1].at[k])
+
+        def half_out(k):
+            r = pl.ds(k * (whole.shape[0] // 2), whole.shape[0] // 2)
+            return pltpu.make_async_copy(outs[-2].at[r, :], outs[5 + k], outs[-1].at[2 + k])
 
         def w_copies(step, slot):
             rows = pl.ds(pl.multiple_of(step * bp, bp), bp)
@@ -180,6 +190,17 @@
                 def _():
                     out_copy(k).start()
 
+            if nw:
+
+                @pl.when(step == 4)
+                def _():
+                    start([half_in(k) for k in range(2)])
+
+                @pl.when(step == 7)
+                def _():
+                    wait([half_in(k) for k in range(2)])
+                    start([half_out(k) for k in range(2)])
+
             wait(w_copies(step, slot))
             acc = lax.dot_general(du[...], wbuf[slot], NT, preferred_element_type=F32)
             own_ref[...] = acc[:half].astype(BF16)
@@ -188,13 +209,15 @@
         @pl.when(i == gsteps + psteps)
         def _():
             wait([out_copy(k) for k in range(3)])
+            if nw:
+                wait([half_out(k) for k in range(2)])
 
     p_block = lambda i: jnp.maximum(i - gsteps - 1, 0)
     return pl.pallas_call(
         kernel,
         grid=(gsteps + 1 + psteps,),
-        in_specs=[ANY] * (nd + 5),
-        out_specs=[pl.BlockSpec((half, bp), lambda i: (0, p_block(i)))] * 2 + [ANY] * 3,
+        in_specs=[ANY] * (nd + 5 + nw),
+        out_specs=[pl.BlockSpec((half, bp), lambda i: (0, p_block(i)))] * 2 + [ANY] * (3 + 2 * nw),
         scratch_shapes=[
             pltpu.VMEM((total, h), BF16),
             pltpu.VMEM((2, bg, h), BF16),
@@ -210,18 +233,20 @@
             pltpu.SemaphoreType.DMA((gsteps + 1, 2, npc)),
             pltpu.SemaphoreType.DMA((3,)),
             pltpu.SemaphoreType.DMA((2, 2)),
-        ],
+        ]
+        + ([pltpu.VMEM(whole.shape, BF16), pltpu.SemaphoreType.DMA((4,))] if nw else []),
         out_shape=[
             jax.ShapeDtypeStruct((half, h), BF16),
             jax.ShapeDtypeStruct((half, h), BF16),
             jax.ShapeDtypeStruct((total, f), BF16),
             jax.ShapeDtypeStruct((total, f), BF16),
             jax.ShapeDtypeStruct((f, total), BF16),
-        ],
+        ]
+        + [jax.ShapeDtypeStruct((whole.shape[0] // 2, whole.shape[1]), BF16) for _ in range(2 * nw)],
         compiler_params=params(),
         cost_estimate=cost(total, 3 * h, f, 2 * (3 * f * h + total * (2 * h + 5 * f))),
         name="gp_chunk",
-    )(*dys, wd, ug, uu, wg, wu)
+    )(*dys, wd, ug, uu, wg, wu, *([whole] if nw else []))
 
 
 def dw(streamed, moves, resident, transposed, bn):
@@ -331,34 +356,6 @@
     )(*streamed, *[r for group in resident for r in group])
 
 
-def dx_sum(base, rx, ry):
-    t, h = base.shape
-    bc = h // 2
-    u = t // 2
-
-    def kernel(base_ref, rx0, rx1, ry0, ry1, out_ref):
-        for k, (a, b) in enumerate(((rx0, ry0), (rx1, ry1))):
-
-            @pl.when(pl.program_id(0) == k)
-            def _():
-                total = base_ref[...].astype(F32) + a[...].astype(F32) + b[...].astype(F32)
-                out_ref[...] = total.astype(BF16)
-
-    first = pl.BlockSpec((u, bc), lambda i, j: (0, jnp.where(i == 0, j, 1)))
-    second = pl.BlockSpec((u, bc), lambda i, j: (0, jnp.where(i == 1, j, 0)))
-    both = pl.BlockSpec((u, bc), lambda i, j: (i, j))
-    return pl.pallas_call(
-        kernel,
-        grid=(2, 2),
-        in_specs=[both, first, second, first, second],
-        out_specs=both,
-        out_shape=jax.ShapeDtypeStruct((t, h), BF16),
-        compiler_params=params(),
-        cost_estimate=cost(t, 2, h, 8 * t * h),
-        name="dx_sum",
-    )(base, *rx, *ry)
-
-
 def solution(mesh):
     tok = P(("dp", "tp"), None)
     col = P(None, "tp")
@@ -387,7 +384,8 @@
         dyd0, dyd1 = send(dyx0, yn), send(dyy1, xn)
         dyxc1, dyyc0 = send(dyx1, core), send(dyy0, core)
         dydc0, dydc1 = send(dyd0, core), send(dyd1, core)
-        xp = [x[:u], x[u:]]
+        *first, xa, xb = gp_chunk([dy, dyc], wd, ug, uu, wg, wu, [(0, 0, t), (1, 0, t)], whole=x)
+        xp = [xa, xb]
         xc = send(x, core)
         xx0, xy1 = send(xp[0], xn), send(xp[1], yn)
         xx1, xy0 = send(xp[1], xn), send(xp[0], yn)
@@ -403,8 +401,10 @@
             ([dyd0, dyd1, dydc0, dydc1], [(6, 0, t), (7, 0, t)]),
         )
         own, oth, dug, duu, zt = [], [], [], [], []
-        for rows, places in chunks:
-            res = gp_chunk(rows, wd, ug, uu, wg, wu, places)
+        for c, (rows, places) in enumerate(chunks):
+            res = first
+            if c:
+                res = gp_chunk(rows, wd, ug, uu, wg, wu, places)
             for dst, r in zip((own, oth, dug, duu, zt), res):
                 dst.append(r)
         got = [send(oth[c], core) for c in range(4)]
@@ -416,7 +416,7 @@
         rx1 = send(add(*mine(2, 0), rdy), xn)
         ry0 = send(add(*mine(2, 1), rdx), yn)
         base = add(own[0], got[0])
-        dx = dx_sum(base, (rx0, rx1), (ry0, ry1))
+        dx = jnp.concatenate([add(base[:u], rx0, ry0), add(base[u:], rx1, ry1)])
 
         def moves(parts):
             out, dst = [], 0

time: 633 us -> 610 us (0.964)
  waiting for transfers between devices: 149 us -> 133 us
  Pallas kernels: 419 us -> 411 us
    ppermute x36, waiting for transfers between devices: 149 us -> 133 us  [send(): return lax.ppermute(a, 'tp', to)]
    pallas_call x1 -> x0, Pallas kernels: 7.32 us -> none  [dx_sum(): pl.pallas_call(kernel, grid=(2, 2), in_specs=[both, first, second, first,...]
    convert_element_type x4 -> x5, other arithmetic: 23.5 us -> 25.9 us  [add(): functools.reduce(lambda a, b: a + b, [t.astype(F32) for t in terms])]
  transfers between devices with their start and end apart: 36 -> 36, of which waited for: 6 -> 5; matrix products, arithmetic and copies ran while one was open for 4% -> 4% of each run, Pallas kernels for 66% -> 68%
where the time goes in v3:
time: 610 us; the launch traced here: 603 us
  Pallas kernels  411 us (67%)
  waiting for transfers between devices  133 us (22%)
  other arithmetic  28.1 us (5%)
  starting transfers between devices  23.4 us (4%)
    pallas_call x4, Pallas kernels, gp_chunk(): pl.pallas_call(kernel, grid=(gsteps + 1 + psteps,), in_specs=[ANY] * (nd...  220 us
    pallas_call x2, Pallas kernels, dw(): pl.pallas_call(kernel, grid=(steps,), in_specs=[ANY] * (ns + nr), out_spe...  192 us
    ppermute x36, waiting for transfers between devices, send(): return lax.ppermute(a, 'tp', to)  133 us
    convert_element_type x5, other arithmetic, add(): functools.reduce(lambda a, b: a + b, [t.astype(F32) for t in terms])  25.9 us
    ppermute x36, starting transfers between devices, send(): return lax.ppermute(a, 'tp', to)  23.4 us
  transfers between devices with their start and end apart: 36, of which 5 were waited for; matrix products, arithmetic and copies ran while one was open for 4% of the time, Pallas kernels for 68%

profile of v3, /device:TPU:0, one launch (start us, length us, event | category | flops | bytes accessed | tf_op | source)
XLA Modules:
  0.0 603.1 jit_solution(15189611301426669713)
XLA Ops:
  0.6 0.9 collective-permute-start
  1.5 2.4 fusion
  3.9 2.5 collective-permute-start.3
  6.4 1.5 collective-permute-start.8
  8.5 41.6 %collective-permute-done.3.refs_1_.refs_3_ = bf16[192,5120]{1,0:T(8,128)(2,1)S(1)} collective-permute-done((bf16[192,5120]{1,0:T(8,128)(2,1)S(1)}, bf16[192,5120]{1,0:T(8,128)(2,1)S(1)}, u32[]{:S(2)}, u32[]{:S(2)}) %collective-permute-start.3) | collective-permute-done | bytes 1966112 | tf_op jit(solution)/shard_map/ppermute | solution.py:369
  50.1 2.0 collective-permute-start.14
  52.1 42.2 %collective-permute-done.2.refs_0_.refs_2_ = bf16[192,5120]{1,0:T(8,128)(2,1)} collective-permute-done((bf16[192,5120]{1,0:T(8,128)(2,1)S(1)}, bf16[192,5120]{1,0:T(8,128)(2,1)}, u32[]{:S(2)}, u32[]{:S(2)}) %collective-permute-start.2) | collective-permute-done | bytes 1966112 | tf_op jit(solution)/shard_map/ppermute | solution.py:369
  94.4 54.3 %gp_chunk.4 = (bf16[384,5120]{1,0:T(8,128)(2,1)}, bf16[384,5120]{1,0:T(8,128)(2,1)}, bf16[768,1792]{1,0:T(8,128)(2,1)}, bf16[768,1792]{1,0:T(8,128)(2,1)}, bf16[...) custom-call(bf16[384,5120]{1,0:T(8,128)(2,1)} %refs_0_.5, ...), custom_call_target="tpu_custom_call" | custom-call | flops 42278584320 | bytes 84541440 | tf_op jit(solution)/shard_map/gp_chunk/pallas_call | solution.py:216
  150.3 55.3 %gp_chunk.5 = (bf16[384,5120]{1,0:T(8,128)(2,1)}, bf16[384,5120]{1,0:T(8,128)(2,1)}, bf16[768,1792]{1,0:T(8,128)(2,1)}, bf16[768,1792]{1,0:T(8,128)(2,1)}, bf16[1792,768]{1,0:T(8,128)(2,1)}) custom-call(bf16[192,5120]{1,0:T(8,128)(2,1)} %collective-permute-done.2.refs_0_.refs_2_, bf16[192,5120]{1,0:T(8,128)(2,1)} %copy-done.4, ...), custom_call_target="tpu_custom_call" | custom-call | flops 42278584320 | bytes 84541440 | tf_op jit(solution)/shard_map/gp_chunk/pallas_call | solution.py:216
  205.6 2.0 collective-permute-start.29
  207.6 1.5 collective-permute-start.24
  209.1 54.8 %gp_chunk.7 = (bf16[384,5120]{1,0:T(8,128)(2,1)}, bf16[384,5120]{1,0:T(8,128)(2,1)}, bf16[768,1792]{1,0:T(8,128)(2,1)}, bf16[768,1792]{1,0:T(8,128)(2,1)}, bf16[1792,768]{1,0:T(8,128)(2,1)}) custom-call(bf16[192,5120]{1,0:T(8,128)(2,1)} %collective-permute-done.13.refs_0_.refs_10_, bf16[192,5120]{1,0:T(8,128)(2,1)} %collective-permute-done.14.refs_1_.refs_11_, ...), custom_call_target="tpu_custom_call" | custom-call | flops 42278584320 | bytes 84541440 | tf_op jit(solution)/shard_map/gp_chunk/pallas_call | solution.py:216
  264.0 1.2 copy-done.8
  265.7 55.2 %gp_chunk.6 = (bf16[384,5120]{1,0:T(8,128)(2,1)}, bf16[384,5120]{1,0:T(8,128)(2,1)}, bf16[768,1792]{1,0:T(8,128)(2,1)}, bf16[768,1792]{1,0:T(8,128)(2,1)}, bf16[1792,768]{1,0:T(8,128)(2,1)}) custom-call(bf16[192,5120]{1,0:T(8,128)(2,1)} %copy-done.5, bf16[192,5120]{1,0:T(8,128)(2,1)} %collective-permute-done.9.refs_1_.refs_7_, bf16[192,5120]{1,0:T(8,128)(2,1)} %copy-done.8, ...), custom_call_target="tpu_custom_call" | custom-call | flops 42278584320 | bytes 84541440 | tf_op jit(solution)/shard_map/gp_chunk/pallas_call | solution.py:216
  322.7 6.7 %add_convert_fusion.7 = (bf16[192,5120]{1,0:T(8,128)(2,1)}, bf16[192,5120]{1,0:T(8,128)(2,1)}) fusion(bf16[384,5120]{1,0:T(8,128)(2,1)} %collective-permute-done.17, bf16[384,5120]{1,0:T(8,128)(2,1)} %get-tuple-element.34), kind=kLoop, calls=%fused_computation.8 | loop fusion | flops 7864320 | bytes 11796480 | tf_op jit(solution)/shard_map/convert_element_type | solution.py:372
  329.4 37.1 %collective-permute-done.28.refs_6_ = bf16[192,5120]{1,0:T(8,128)(2,1)S(1)} collective-permute-done((bf16[192,5120]{1,0:T(8,128)(2,1)}, bf16[192,5120]{1,0:T(8,128)(2,1)S(1)}, u32[]{:S(2)}, u32[]{:S(2)}) %collective-permute-start.28) | collective-permute-done | bytes 1966112 | tf_op jit(solution)/shard_map/ppermute | solution.py:369
  366.8 0.7 collective-permute-start.32
  367.7 1.1 collective-permute-start.33
  368.8 0.9 collective-permute-start.18
  369.7 1.1 collective-permute-start.20
  370.9 66.0 %dw.3 = f32[1792,5120]{1,0:T(8,128)} custom-call(bf16[384,5120]{1,0:T(8,128)(2,1)} %refs_0_.5, bf16[384,5120]{1,0:T(8,128)(2,1)} %collective-permute-done.refs_1_, bf16[192,5120]{1,0:T(8,128)(2,1)} %collective-permute-done.2.refs_0_.refs_2_, bf16[192,5120]{1,0:T(8,128)(2,1)} %copy-done.4, bf16[192,5120]{1,0:T(8,128)(2,1)} %collective-permute-done.4.refs_2_.refs_4_, ...), custom_call_target="tpu_custom_call" | custom-call | flops 56371445760 | bytes 79167488 | tf_op jit(solution)/shard_map/dw/pallas_call | solution.py:341
  437.0 4.9 add_convert_fusion
  442.5 11.9 %collective-permute-done.18 = bf16[192,5120]{1,0:T(8,128)(2,1)} collective-permute-done((bf16[192,5120]{1,0:T(8,128)(2,1)}, bf16[192,5120]{1,0:T(8,128)(2,1)}, u32[]{:S(2)}, u32[]{:S(2)}) %collective-permute-start.18) | collective-permute-done | bytes 1966112 | tf_op jit(solution)/shard_map/ppermute | solution.py:369
  454.9 3.5 add_convert_fusion.8
  458.4 5.5 add_convert_fusion.6
  464.0 0.8 collective-permute-start.7
  465.2 1.3 copy-done.11
  466.5 1.5 collective-permute-start.22
  468.6 0.8 collective-permute-start.21
  469.4 125.8 %dw.2 = (f32[5120,1792]{1,0:T(8,128)}, f32[5120,1792]{1,0:T(8,128)}) custom-call(bf16[384,5120]{1,0:T(8,128)(2,1)} %refs_0_.4, bf16[384,5120]{1,0:T(8,128)(2,1)} %collective-permute-done.23.refs_1_, bf16[192,5120]{1,0:T(8,128)(2,1)} %collective-permute-done.24.refs_2_, bf16[192,5120]{1,0:T(8,128)(2,1)} %collective-permute-done.25.refs_3_, ...), custom_call_target="tpu_custom_call" | custom-call | flops 112742891520 | bytes 126877696 | tf_op jit(solution)/shard_map/dw/pallas_call | solution.py:341
  595.2 5.3 add_convert_fusion.5
  600.5 2.2 pad_maximum_fusion
  (77 shorter events, 7.1 us)
Async XLA Ops:
  0.6 93.8 %collective-permute-start = (bf16[384,5120]{1,0:T(8,128)(2,1)}, bf16[384,5120]{1,0:T(8,128)(2,1)}, u32[]{:S(2)}, u32[]{:S(2)}) collective-permute-start(bf16[384,5120]{1,0:T(8,128)(2,1)} %refs_0_.5), channel_id=1, source_target_pairs={{0,1},{1,0},{2,3},{3,2},{4,5},{5,4},{6,7},{7,6}} | collective-permute-start | bytes 11796488 | tf_op jit(solution)/shard_map/ppermute | solution.py:369
  3.9 46.2 %collective-permute-start.3 = (bf16[192,5120]{1,0:T(8,128)(2,1)S(1)}, bf16[192,5120]{1,0:T(8,128)(2,1)S(1)}, u32[]{:S(2)}, u32[]{:S(2)}) collective-permute-start(bf16[192,5120]{1,0:T(8,128)(2,1)S(1)} %get-tuple-element.60), channel_id=1, source_target_pairs={{0,4},{1,5},{2,6},{3,7},{4,0},{5,1},{6,2},{7,3}} | collective-permute-start | bytes 5898248 | tf_op jit(solution)/shard_map/ppermute | solution.py:369
  6.4 45.7 %collective-permute-start.8 = (bf16[192,5120]{1,0:T(8,128)(2,1)S(1)}, bf16[192,5120]{1,0:T(8,128)(2,1)S(1)}, u32[]{:S(2)}, u32[]{:S(2)}) collective-permute-start(bf16[192,5120]{1,0:T(8,128)(2,1)S(1)} %get-tuple-element.60), channel_id=1, source_target_pairs={{0,2},{1,3},{2,0},{3,1},{4,6},{5,7},{6,4},{7,5}} | collective-permute-start | bytes 5898248 | tf_op jit(solution)/shard_map/ppermute | solution.py:369
  7.9 86.4 %collective-permute-start.2 = (bf16[192,5120]{1,0:T(8,128)(2,1)S(1)}, bf16[192,5120]{1,0:T(8,128)(2,1)}, u32[]{:S(2)}, u32[]{:S(2)}) collective-permute-start(bf16[192,5120]{1,0:T(8,128)(2,1)S(1)} %get-tuple-element.61), channel_id=1, source_target_pairs={{0,2},{1,3},{2,0},{3,1},{4,6},{5,7},{6,4},{7,5}} | collective-permute-start | bytes 5898248 | tf_op jit(solution)/shard_map/ppermute | solution.py:369
  8.4 140.3 %collective-permute-start.9 = (bf16[192,5120]{1,0:T(8,128)(2,1)S(1)}, bf16[192,5120]{1,0:T(8,128)(2,1)}, u32[]{:S(2)}, u32[]{:S(2)}) collective-permute-start(bf16[192,5120]{1,0:T(8,128)(2,1)S(1)} %get-tuple-element.61), channel_id=1, source_target_pairs={{0,4},{1,5},{2,6},{3,7},{4,0},{5,1},{6,2},{7,3}} | collective-permute-start | bytes 5898248 | tf_op jit(solution)/shard_map/ppermute | solution.py:369
  50.1 99.2 %collective-permute-start.14 = (bf16[192,5120]{1,0:T(8,128)(2,1)S(1)}, bf16[192,5120]{1,0:T(8,128)(2,1)}, u32[]{:S(2)}, u32[]{:S(2)}) collective-permute-start(bf16[192,5120]{1,0:T(8,128)(2,1)S(1)} %collective-permute-done.3.refs_1_.refs_3_), channel_id=1, source_target_pairs={{0,2},{1,3},{2,0},{3,1},{4,6},{5,7},{6,4},{7,5}} | collective-permute-start | bytes 5898248 | tf_op jit(solution)/shard_map/ppermute | solution.py:369
  52.1 97.2 %collective-permute-start.5 = (bf16[192,5120]{1,0:T(8,128)(2,1)S(1)}, bf16[192,5120]{1,0:T(8,128)(2,1)}, u32[]{:S(2)}, u32[]{:S(2)}) collective-permute-start(bf16[192,5120]{1,0:T(8,128)(2,1)S(1)} %collective-permute-done.3.refs_1_.refs_3_), channel_id=1, source_target_pairs={{0,1},{1,0},{2,3},{3,2},{4,5},{5,4},{6,7},{7,6}} | collective-permute-start | bytes 5898248 | tf_op jit(solution)/shard_map/ppermute | solution.py:369
  94.4 55.4 %collective-permute-start.13 = (bf16[192,5120]{1,0:T(8,128)(2,1)}, bf16[192,5120]{1,0:T(8,128)(2,1)}, u32[]{:S(2)}, u32[]{:S(2)}) collective-permute-start(bf16[192,5120]{1,0:T(8,128)(2,1)} %collective-permute-done.2.refs_0_.refs_2_), channel_id=1, source_target_pairs={{0,4},{1,5},{2,6},{3,7},{4,0},{5,1},{6,2},{7,3}} | collective-permute-start | bytes 5898248 | tf_op jit(solution)/shard_map/ppermute | solution.py:369
  94.4 55.4 %collective-permute-start.4 = (bf16[192,5120]{1,0:T(8,128)(2,1)}, bf16[192,5120]{1,0:T(8,128)(2,1)}, u32[]{:S(2)}, u32[]{:S(2)}) collective-permute-start(bf16[192,5120]{1,0:T(8,128)(2,1)} %collective-permute-done.2.refs_0_.refs_2_), channel_id=1, source_target_pairs={{0,1},{1,0},{2,3},{3,2},{4,5},{5,4},{6,7},{7,6}} | collective-permute-start | bytes 5898248 | tf_op jit(solution)/shard_map/ppermute | solution.py:369
  148.8 172.2 %collective-permute-start.23 = (bf16[384,5120]{1,0:T(8,128)(2,1)}, bf16[384,5120]{1,0:T(8,128)(2,1)}, u32[]{:S(2)}, u32[]{:S(2)}) collective-permute-start(bf16[384,5120]{1,0:T(8,128)(2,1)} %refs_0_.4), channel_id=1, source_target_pairs={{0,1},{1,0},{2,3},{3,2},{4,5},{5,4},{6,7},{7,6}} | collective-permute-start | bytes 11796488 | tf_op jit(solution)/shard_map/ppermute | solution.py:369
  149.3 114.7 %collective-permute-start.10 = (bf16[192,5120]{1,0:T(8,128)(2,1)}, bf16[192,5120]{1,0:T(8,128)(2,1)S(1)}, u32[]{:S(2)}, u32[]{:S(2)}) collective-permute-start(bf16[192,5120]{1,0:T(8,128)(2,1)} %copy-done.5), channel_id=1, source_target_pairs={{0,1},{1,0},{2,3},{3,2},{4,5},{5,4},{6,7},{7,6}} | collective-permute-start | bytes 5898248 | tf_op jit(solution)/shard_map/ppermute | solution.py:369
  149.3 115.9 %collective-permute-start.11 = (bf16[192,5120]{1,0:T(8,128)(2,1)}, bf16[192,5120]{1,0:T(8,128)(2,1)}, u32[]{:S(2)}, u32[]{:S(2)}) collective-permute-start(bf16[192,5120]{1,0:T(8,128)(2,1)} %collective-permute-done.9.refs_1_.refs_7_), channel_id=1, source_target_pairs={{0,1},{1,0},{2,3},{3,2},{4,5},{5,4},{6,7},{7,6}} | collective-permute-start | bytes 5898248 | tf_op jit(solution)/shard_map/ppermute | solution.py:369
  149.8 55.8 %collective-permute-start.16 = (bf16[192,5120]{1,0:T(8,128)(2,1)}, bf16[192,5120]{1,0:T(8,128)(2,1)S(1)}, u32[]{:S(2)}, u32[]{:S(2)}) collective-permute-start(bf16[192,5120]{1,0:T(8,128)(2,1)} %collective-permute-done.14.refs_1_.refs_11_), channel_id=1, source_target_pairs={{0,1},{1,0},{2,3},{3,2},{4,5},{5,4},{6,7},{7,6}} | collective-permute-start | bytes 5898248 | tf_op jit(solution)/shard_map/ppermute | solution.py:369
  149.8 57.8 %collective-permute-start.15 = (bf16[192,5120]{1,0:T(8,128)(2,1)}, bf16[192,5120]{1,0:T(8,128)(2,1)}, u32[]{:S(2)}, u32[]{:S(2)}) collective-permute-start(bf16[192,5120]{1,0:T(8,128)(2,1)} %collective-permute-done.13.refs_0_.refs_10_), channel_id=1, source_target_pairs={{0,1},{1,0},{2,3},{3,2},{4,5},{5,4},{6,7},{7,6}} | collective-permute-start | bytes 5898248 | tf_op jit(solution)/shard_map/ppermute | solution.py:369
  205.6 115.4 %collective-permute-start.29 = (bf16[192,5120]{1,0:T(8,128)(2,1)}, bf16[192,5120]{1,0:T(8,128)(2,1)}, u32[]{:S(2)}, u32[]{:S(2)}) collective-permute-start(bf16[192,5120]{1,0:T(8,128)(2,1)} %get-tuple-element.36), channel_id=1, source_target_pairs={{0,4},{1,5},{2,6},{3,7},{4,0},{5,1},{6,2},{7,3}} | collective-permute-start | bytes 5898248 | tf_op jit(solution)/shard_map/ppermute | solution.py:369
  207.6 113.8 %collective-permute-start.24 = (bf16[192,5120]{1,0:T(8,128)(2,1)}, bf16[192,5120]{1,0:T(8,128)(2,1)}, u32[]{:S(2)}, u32[]{:S(2)}) collective-permute-start(bf16[192,5120]{1,0:T(8,128)(2,1)} %get-tuple-element.36), channel_id=1, source_target_pairs={{0,2},{1,3},{2,0},{3,1},{4,6},{5,7},{6,4},{7,5}} | collective-permute-start | bytes 5898248 | tf_op jit(solution)/shard_map/ppermute | solution.py:369
  265.2 102.3 %collective-permute-start.6 = (bf16[384,5120]{1,0:T(8,128)(2,1)}, bf16[384,5120]{1,0:T(8,128)(2,1)S(1)}, u32[]{:S(2)}, u32[]{:S(2)}) collective-permute-start(bf16[384,5120]{1,0:T(8,128)(2,1)} %get-tuple-element.31), channel_id=1, source_target_pairs={{0,1},{1,0},{2,3},{3,2},{4,5},{5,4},{6,7},{7,6}} | collective-permute-start | bytes 11796488 | tf_op jit(solution)/shard_map/ppermute | solution.py:369
  265.2 56.8 %collective-permute-start.17 = (bf16[384,5120]{1,0:T(8,128)(2,1)}, bf16[384,5120]{1,0:T(8,128)(2,1)}, u32[]{:S(2)}, u32[]{:S(2)}) collective-permute-start(bf16[384,5120]{1,0:T(8,128)(2,1)} %get-tuple-element.35), channel_id=1, source_target_pairs={{0,1},{1,0},{2,3},{3,2},{4,5},{5,4},{6,7},{7,6}} | collective-permute-start | bytes 11796488 | tf_op jit(solution)/shard_map/ppermute | solution.py:369
  320.9 47.9 %collective-permute-start.12 = (bf16[384,5120]{1,0:T(8,128)(2,1)}, bf16[384,5120]{1,0:T(8,128)(2,1)}, u32[]{:S(2)}, u32[]{:S(2)}) collective-permute-start(bf16[384,5120]{1,0:T(8,128)(2,1)} %get-tuple-element.33), channel_id=1, source_target_pairs={{0,1},{1,0},{2,3},{3,2},{4,5},{5,4},{6,7},{7,6}} | collective-permute-start | bytes 11796488 | tf_op jit(solution)/shard_map/ppermute | solution.py:369
  321.0 48.8 %collective-permute-start.1 = (bf16[384,5120]{1,0:T(8,128)(2,1)}, bf16[384,5120]{1,0:T(8,128)(2,1)}, u32[]{:S(2)}, u32[]{:S(2)}) collective-permute-start(bf16[384,5120]{1,0:T(8,128)(2,1)} %get-tuple-element.29), channel_id=1, source_target_pairs={{0,1},{1,0},{2,3},{3,2},{4,5},{5,4},{6,7},{7,6}} | collective-permute-start | bytes 11796488 | tf_op jit(solution)/shard_map/ppermute | solution.py:369
  321.5 45.0 %collective-permute-start.28 = (bf16[192,5120]{1,0:T(8,128)(2,1)}, bf16[192,5120]{1,0:T(8,128)(2,1)S(1)}, u32[]{:S(2)}, u32[]{:S(2)}) collective-permute-start(bf16[192,5120]{1,0:T(8,128)(2,1)} %get-tuple-element.37), channel_id=1, source_target_pairs={{0,2},{1,3},{2,0},{3,1},{4,6},{5,7},{6,4},{7,5}} | collective-permute-start | bytes 5898248 | tf_op jit(solution)/shard_map/ppermute | solution.py:369
  322.0 44.8 %collective-permute-start.25 = (bf16[192,5120]{1,0:T(8,128)(2,1)}, bf16[192,5120]{1,0:T(8,128)(2,1)}, u32[]{:S(2)}, u32[]{:S(2)}) collective-permute-start(bf16[192,5120]{1,0:T(8,128)(2,1)} %get-tuple-element.37), channel_id=1, source_target_pairs={{0,4},{1,5},{2,6},{3,7},{4,0},{5,1},{6,2},{7,3}} | collective-permute-start | bytes 5898248 | tf_op jit(solution)/shard_map/ppermute | solution.py:369
  366.4 75.5 %collective-permute-start.31 = (bf16[192,5120]{1,0:T(8,128)(2,1)}, bf16[192,5120]{1,0:T(8,128)(2,1)}, u32[]{:S(2)}, u32[]{:S(2)}) collective-permute-start(bf16[192,5120]{1,0:T(8,128)(2,1)} %collective-permute-done.29.refs_7_), channel_id=1, source_target_pairs={{0,1},{1,0},{2,3},{3,2},{4,5},{5,4},{6,7},{7,6}} | collective-permute-start | bytes 5898248 | tf_op jit(solution)/shard_map/ppermute | solution.py:369
  366.8 75.2 %collective-permute-start.32 = (bf16[192,5120]{1,0:T(8,128)(2,1)}, bf16[192,5120]{1,0:T(8,128)(2,1)}, u32[]{:S(2)}, u32[]{:S(2)}) collective-permute-start(bf16[192,5120]{1,0:T(8,128)(2,1)} %collective-permute-done.24.refs_2_), channel_id=1, source_target_pairs={{0,4},{1,5},{2,6},{3,7},{4,0},{5,1},{6,2},{7,3}} | collective-permute-start | bytes 5898248 | tf_op jit(solution)/shard_map/ppermute | solution.py:369
  367.7 74.7 %collective-permute-start.33 = (bf16[192,5120]{1,0:T(8,128)(2,1)}, bf16[192,5120]{1,0:T(8,128)(2,1)}, u32[]{:S(2)}, u32[]{:S(2)}) collective-permute-start(bf16[192,5120]{1,0:T(8,128)(2,1)} %collective-permute-done.25.refs_3_), channel_id=1, source_target_pairs={{0,2},{1,3},{2,0},{3,1},{4,6},{5,7},{6,4},{7,5}} | collective-permute-start | bytes 5898248 | tf_op jit(solution)/shard_map/ppermute | solution.py:369
  368.8 85.6 %collective-permute-start.18 = (bf16[192,5120]{1,0:T(8,128)(2,1)}, bf16[192,5120]{1,0:T(8,128)(2,1)}, u32[]{:S(2)}, u32[]{:S(2)}) collective-permute-start(bf16[192,5120]{1,0:T(8,128)(2,1)} %get-tuple-element.56), channel_id=1, source_target_pairs={{0,2},{1,3},{2,0},{3,1},{4,6},{5,7},{6,4},{7,5}} | collective-permute-start | bytes 5898248 | tf_op jit(solution)/shard_map/ppermute | solution.py:369
  369.7 84.6 %collective-permute-start.20 = (bf16[192,5120]{1,0:T(8,128)(2,1)}, bf16[192,5120]{1,0:T(8,128)(2,1)}, u32[]{:S(2)}, u32[]{:S(2)}) collective-permute-start(bf16[192,5120]{1,0:T(8,128)(2,1)} %get-tuple-element.57), channel_id=1, source_target_pairs={{0,4},{1,5},{2,6},{3,7},{4,0},{5,1},{6,2},{7,3}} | collective-permute-start | bytes 5898248 | tf_op jit(solution)/shard_map/ppermute | solution.py:369
  442.0 26.1 %collective-permute-start.27 = (bf16[192,5120]{1,0:T(8,128)(2,1)}, bf16[192,5120]{1,0:T(8,128)(2,1)}, u32[]{:S(2)}, u32[]{:S(2)}) collective-permute-start(bf16[192,5120]{1,0:T(8,128)(2,1)} %collective-permute-done.25.refs_3_), channel_id=1, source_target_pairs={{0,1},{1,0},{2,3},{3,2},{4,5},{5,4},{6,7},{7,6}} | collective-permute-start | bytes 5898248 | tf_op jit(solution)/shard_map/ppermute | solution.py:369
  464.0 131.2 %collective-permute-start.7 = (bf16[192,5120]{1,0:T(8,128)(2,1)}, bf16[192,5120]{1,0:T(8,128)(2,1)}, u32[]{:S(2)}, u32[]{:S(2)}) collective-permute-start(bf16[192,5120]{1,0:T(8,128)(2,1)} %get-tuple-element.52), channel_id=1, source_target_pairs={{0,2},{1,3},{2,0},{3,1},{4,6},{5,7},{6,4},{7,5}} | collective-permute-start | bytes 5898248 | tf_op jit(solution)/shard_map/ppermute | solution.py:369
  466.5 128.7 %collective-permute-start.22 = (bf16[192,5120]{1,0:T(8,128)(2,1)}, bf16[192,5120]{1,0:T(8,128)(2,1)}, u32[]{:S(2)}, u32[]{:S(2)}) collective-permute-start(bf16[192,5120]{1,0:T(8,128)(2,1)} %get-tuple-element.53), channel_id=1, source_target_pairs={{0,4},{1,5},{2,6},{3,7},{4,0},{5,1},{6,2},{7,3}} | collective-permute-start | bytes 5898248 | tf_op jit(solution)/shard_map/ppermute | solution.py:369
  468.1 127.1 %collective-permute-start.19 = (bf16[192,5120]{1,0:T(8,128)(2,1)}, bf16[192,5120]{1,0:T(8,128)(2,1)}, u32[]{:S(2)}, u32[]{:S(2)}) collective-permute-start(bf16[192,5120]{1,0:T(8,128)(2,1)} %get-tuple-element.54), channel_id=1, source_target_pairs={{0,4},{1,5},{2,6},{3,7},{4,0},{5,1},{6,2},{7,3}} | collective-permute-start | bytes 5898248 | tf_op jit(solution)/shard_map/ppermute | solution.py:369
  468.6 126.7 %collective-permute-start.21 = (bf16[192,5120]{1,0:T(8,128)(2,1)}, bf16[192,5120]{1,0:T(8,128)(2,1)}, u32[]{:S(2)}, u32[]{:S(2)}) collective-permute-start(bf16[192,5120]{1,0:T(8,128)(2,1)} %get-tuple-element.55), channel_id=1, source_target_pairs={{0,2},{1,3},{2,0},{3,1},{4,6},{5,7},{6,4},{7,5}} | collective-permute-start | bytes 5898248 | tf_op jit(solution)/shard_map/ppermute | solution.py:369
  (16 other events, 337.1 us)
